TPU v7x, 128 devices: a whole 4x4x4 slice. The times are simulated.
128 devices in a mesh: row: 16 (over x_hi, z, core), col: 8 (over x_lo, y).
Axes of the slice: x: 4 (x_hi: 2, x_lo: 2; x = x_hi * 2 + x_lo), y: 4, z: 4, core: 2. Of those that a mesh axis runs over, the one named last changes fastest.
Arguments:
- tokens: bfloat16 [65536, 6144], P(('row', 'col')), may hold values from -6 to 6
- grad_out: bfloat16 [65536, 6144], P(('row', 'col')), may hold values from -6 to 6
- w_up: bfloat16 [6144, 512], replicated, may hold values from -0.078125 to 0.078125
- w_down: bfloat16 [512, 6144], replicated, may hold values from -0.0390625 to 0.0390625
Outputs:
- up_grad: float32 [6144, 512], P('row', 'col')
- down_grad: float32 [6144, 512], P('row', 'col')
All inputs are finite; a program needn't handle non-finite values.
Results may differ from a plain program's by a relative error of at most 0.0041.
Values may be sent and summed in bfloat16 or wider, within the bound.
A program may use at most 128 MiB of HBM per device.

v0:
```python
import math

import jax
import jax.numpy as jnp
from jax import lax
from jax.sharding import PartitionSpec as P


def gelu_parts(preact):
    cumul = 0.5 * (1.0 + jax.scipy.special.erf(preact / math.sqrt(2.0)))
    density = jnp.exp(-0.5 * preact * preact) / math.sqrt(2.0 * math.pi)
    return (preact * cumul, cumul + preact * density)


def reduce_bucket(term):
    levels = term.astype(jnp.bfloat16)
    rows, cols = levels.shape
    row_count = lax.axis_size("row")
    col_count = lax.axis_size("col")
    piece_rows = rows // row_count
    piece_cols = cols // col_count
    owners = row_count * col_count
    level_blocks = (
        levels.reshape(row_count, piece_rows, col_count, piece_cols)
        .transpose(0, 2, 1, 3)
        .reshape(owners, piece_rows, piece_cols)
    )
    got_levels = lax.all_to_all(
        level_blocks, ("row", "col"), split_axis=0, concat_axis=0, tiled=True
    )
    return jnp.sum(got_levels, axis=0, dtype=jnp.float32)


def local(tokens, grad_out, w_up, w_down):
    preact = jnp.dot(tokens, w_up, preferred_element_type=jnp.float32)
    act_grad = lax.dot_general(
        grad_out, w_down, (((1,), (1,)), ((), ())), preferred_element_type=jnp.float32
    )
    value, slope = gelu_parts(preact)
    act = value.astype(jnp.bfloat16)
    hidden_grad = (act_grad * slope).astype(jnp.bfloat16)
    term_up = lax.dot_general(
        tokens, hidden_grad, (((0,), (0,)), ((), ())), preferred_element_type=jnp.float32
    )
    summed_up = reduce_bucket(term_up)
    term_down = lax.dot_general(
        grad_out, act, (((0,), (0,)), ((), ())), preferred_element_type=jnp.float32
    )
    summed_down = reduce_bucket(term_down)
    total_tokens = tokens.shape[0] * lax.axis_size("row") * lax.axis_size("col")
    factor = 1.0 / math.sqrt(total_tokens)
    return (summed_up * factor, summed_down * factor)


def solution(mesh):
    placed = (P(("row", "col"), None), P(("row", "col"), None), P(), P())
    return jax.shard_map(
        local,
        mesh=mesh,
        in_specs=placed,
        out_specs=(P("row", "col"), P("row", "col")),
        check_vma=False,
    )
```

profile of v0, /device:TPU:17, one launch (start us, length us, event | category | flops | bytes accessed | tf_op | source)
XLA Modules:
  0.0 201.3 jit_solution(16235122465278878615)
XLA Ops:
  0.6 0.0 copy-start
  0.6 7.6 %fusion.9 = f32[512,512]{1,0:T(8,128)S(1)} fusion(bf16[512,6144]{1,0:T(8,128)(2,1)} %param.4, bf16[6144,512]{1,0:T(8,128)(2,1)} %param.6), kind=kOutput, calls=%fused_computation.19 | convolution fusion | flops 3221225472 | bytes 13631488 | tf_op jit(solution)/shard_map/dot_general | solution.py:35
  8.2 0.0 copy-done
  8.3 3.9 %convolution_convert_fusion = bf16[512,6144]{1,0:T(8,128)(2,1)S(1)} fusion(bf16[512,6144]{1,0:T(8,128)(2,1)S(1)} %copy-done, f32[512,512]{1,0:T(8,128)S(1)} %fusion.9), kind=kOutput, calls=%fused_computation.2 | convolution fusion | flops 3225681920 | bytes 13631488 | tf_op jit(solution)/shard_map/dot_general | solution.py:46
  12.2 1.6 copy.9
  13.8 4.2 %copy.7 = bf16[16,384,8,64]{1,3,2,0:T(8,128)(2,1)} copy(bf16[16,384,8,64]{1,0,3,2:T(8,128)(2,1)S(1)} %bitcast.26) | data formatting | bytes 12582912 | tf_op jit(solution)/shard_map/reshape | solution.py:24
  18.1 11.0 %all-to-all-start.1 = ((bf16[128,384,64]{1,2,0:T(8,128)(2,1)}), bf16[128,384,64]{1,2,0:T(8,128)(2,1)}, u32[]{:S(2)}, u32[]{:S(2)}) async-start(bf16[128,384,64]{1,2,0:T(8,128)(2,1)} %bitcast.25), calls=%async_computation.1 | async-start | bytes 12582912 | tf_op jit(solution)/shard_map/all_to_all | solution.py:28
  29.1 16.0 %convolution_convert_fusion.1 = bf16[512,6144]{1,0:T(8,128)(2,1)} fusion(bf16[512,6144]{1,0:T(8,128)(2,1)} %param.4, bf16[512,6144]{1,0:T(8,128)(2,1)} %param.5, bf16[512,6144]{1,0:T(8,128)(2,1)} %param.7, f32[512,512]{1,0:T(8,128)S(1)} %fusion.9), kind=kOutput, calls=%fused_computation.3 | convolution fusion | flops 6448218112 | bytes 26214400 | tf_op jit(solution)/shard_map/dot_general | solution.py:42
  45.1 4.4 %copy.8 = bf16[64,8,16,384]{3,2,1,0:T(8,128)(2,1)S(1)} copy(bf16[64,8,16,384]{3,1,2,0:T(8,128)(2,1)} %bitcast.29) | data formatting | bytes 12582912
  49.5 4.2 %copy.6 = bf16[16,384,8,64]{1,3,2,0:T(8,128)(2,1)} copy(bf16[16,384,8,64]{1,0,3,2:T(8,128)(2,1)S(1)} %bitcast.27) | data formatting | bytes 12582912 | tf_op jit(solution)/shard_map/reshape | solution.py:24
  53.7 56.3 %all-to-all-done.1 = bf16[128,384,64]{1,2,0:T(8,128)(2,1)} async-done(((bf16[128,384,64]{1,2,0:T(8,128)(2,1)}), bf16[128,384,64]{1,2,0:T(8,128)(2,1)}, u32[]{:S(2)}, u32[]{:S(2)}) %all-to-all-start.1) | async-done | bytes 6291488 | tf_op jit(solution)/shard_map/all_to_all | solution.py:28
  110.0 6.0 %all-to-all-start = ((bf16[128,384,64]{1,2,0:T(8,128)(2,1)}), bf16[128,384,64]{1,2,0:T(8,128)(2,1)}, u32[]{:S(2)}, u32[]{:S(2)}) async-start(bf16[128,384,64]{1,2,0:T(8,128)(2,1)} %bitcast.24), calls=%async_computation | async-start | bytes 12582912 | tf_op jit(solution)/shard_map/all_to_all | solution.py:28
  116.1 3.7 %convert_reduce_fusion = f32[384,64]{0,1:T(8,128)S(1)} fusion(bf16[128,384,64]{1,2,0:T(8,128)(2,1)} %all-to-all-done.1), kind=kLoop, calls=%fused_computation | loop fusion | flops 6266880 | bytes 6389760 | tf_op jit(solution)/shard_map/reduce_sum | solution.py:31
  119.8 0.6 broadcast_multiply_fusion
  120.4 76.5 %all-to-all-done = bf16[128,384,64]{1,2,0:T(8,128)(2,1)} async-done(((bf16[128,384,64]{1,2,0:T(8,128)(2,1)}), bf16[128,384,64]{1,2,0:T(8,128)(2,1)}, u32[]{:S(2)}, u32[]{:S(2)}) %all-to-all-start) | async-done | bytes 6291488 | tf_op jit(solution)/shard_map/all_to_all | solution.py:28
  196.9 3.7 %convert_reduce_fusion.1 = f32[384,64]{0,1:T(8,128)S(1)} fusion(bf16[128,384,64]{1,2,0:T(8,128)(2,1)} %all-to-all-done), kind=kLoop, calls=%fused_computation.1 | loop fusion | flops 6266880 | bytes 6389760 | tf_op jit(solution)/shard_map/reduce_sum | solution.py:31
  200.6 0.6 broadcast_multiply_fusion.1
Async XLA Ops:
  0.6 7.6 %copy-start = (bf16[512,6144]{1,0:T(8,128)(2,1)S(1)}, bf16[512,6144]{1,0:T(8,128)(2,1)}, u32[]{:S(2)}) copy-start(bf16[512,6144]{1,0:T(8,128)(2,1)} %param.5) | copy-start | bytes 18874372
  18.1 91.9 %all-to-all-start.1 = ((bf16[128,384,64]{1,2,0:T(8,128)(2,1)}), bf16[128,384,64]{1,2,0:T(8,128)(2,1)}, u32[]{:S(2)}, u32[]{:S(2)}) async-start(bf16[128,384,64]{1,2,0:T(8,128)(2,1)} %bitcast.25), calls=%async_computation.1 | async-start | bytes 12582912 | tf_op jit(solution)/shard_map/all_to_all | solution.py:28
  110.0 86.9 %all-to-all-start = ((bf16[128,384,64]{1,2,0:T(8,128)(2,1)}), bf16[128,384,64]{1,2,0:T(8,128)(2,1)}, u32[]{:S(2)}, u32[]{:S(2)}) async-start(bf16[128,384,64]{1,2,0:T(8,128)(2,1)} %bitcast.24), calls=%async_computation | async-start | bytes 12582912 | tf_op jit(solution)/shard_map/all_to_all | solution.py:28
where the time goes:
time: 202 us; the launch traced here: 201 us
  waiting for transfers between devices  133 us (66%)
  matrix products  27.5 us (14%)
  starting transfers between devices  17.1 us (8%)
  local copies, waits for them, and re-layouts  14.5 us (7%)
  other arithmetic  8.68 us (4%)
    all_to_all x2, waiting for transfers between devices, reduce_bucket(): lax.all_to_all(level_blocks, ('row', 'col'), split_axis=0, concat_axis=0,...  133 us
    all_to_all x2, starting transfers between devices, reduce_bucket(): lax.all_to_all(level_blocks, ('row', 'col'), split_axis=0, concat_axis=0,...  17.1 us
    dot_general x1, matrix products, local(): lax.dot_general(tokens, hidden_grad, (((0,), (0,)), ((), ())), preferred_...  16 us
    reshape x2, local copies, waits for them, and re-layouts, reduce_bucket(): levels.reshape(row_count, piece_rows, col_count, piece_cols)  8.45 us
    dot_general x1, matrix products, local(): preact = jnp.dot(tokens, w_up, preferred_element_type=jnp.float32)  7.6 us
    reduce_sum x2, other arithmetic, reduce_bucket(): return jnp.sum(got_levels, axis=0, dtype=jnp.float32)  7.39 us
    unnamed x4, local copies, waits for them, and re-layouts  6.08 us
  transfers between devices with their start and end apart: 2, of which 2 were waited for; matrix products, arithmetic and copies ran while one was open for 14% of the time, Pallas kernels for 0%

commit v1 on v0

v1 whole, which is shorter than its diff:
```python
import functools
import math

import jax
import jax.numpy as jnp
from jax import lax
from jax.experimental import pallas as pl
from jax.experimental.pallas import tpu as pltpu
from jax.sharding import PartitionSpec as P

MESH = pl.DeviceIdType.MESH
BF16, F32 = jnp.bfloat16, jnp.float32
ROOT2, ROOT2PI = math.sqrt(2.0), math.sqrt(2.0 * math.pi)
DOWN, UP = 0, 1
TOK, WIDTH, HID = 512, 6144, 512
AHEAD = 3


def remainder(a, n):
    return lax.rem(a, jnp.int32(n))


def kernel(
    factor,
    tok_hbm, grad_hbm, wup_hbm, wdn_hbm,
    up_ref, dn_ref,
    tok, grad, wup, wdn, tok_mate, grad_mate,
    pre, lin, act, act_mate, hid, hid_mate,
    part, own1, far1, got1, send2, own2, far2, got2, send3, got3,
    load_sem, mate_send, mate_recv, out_sem, in_sem,
):
    row, col = lax.axis_index("row"), lax.axis_index("col")
    core = remainder(row, 2)
    at = {
        "x": (row // 8) * 2 + col // 4,
        "y": remainder(col, 4),
        "z": remainder(row // 2, 4),
    }
    mate = (row + 1 - 2 * core, col)

    def peer(axis, shift):
        to = dict(at)
        to[axis] = remainder(at[axis] + shift, 4)
        return ((to["x"] // 2) * 8 + to["z"] * 2 + core, remainder(to["x"], 2) * 4 + to["y"])

    orders = (("x", "y", "z"), ("y", "z", "x"), ("z", "x", "y"))

    barrier = pltpu.get_barrier_semaphore()
    pl.semaphore_signal(barrier, inc=1, device_id=mate, device_id_type=MESH)
    for axis in ("x", "y", "z"):
        for shift in (1, 3, 2):
            pl.semaphore_signal(barrier, inc=1, device_id=peer(axis, shift), device_id_type=MESH)

    def wide(pair, half):
        return pl.ds(pl.multiple_of(pair * 768 + half * 384, 128), 384)

    loads = []
    for pair in range(8):
        loads.append([
            pltpu.make_async_copy(wup_hbm.at[pl.ds(pair * 768, 768), :], wup.at[pair], load_sem.at[pair, 0]),
            pltpu.make_async_copy(tok_hbm.at[:, wide(pair, 0)], tok.at[pair, 0], load_sem.at[pair, 1]),
            pltpu.make_async_copy(tok_hbm.at[:, wide(pair, 1)], tok.at[pair, 1], load_sem.at[pair, 2]),
        ])
    for pair in range(8):
        loads.append([
            pltpu.make_async_copy(grad_hbm.at[:, wide(pair, 0)], grad.at[pair, 0], load_sem.at[8 + pair, 0]),
            pltpu.make_async_copy(grad_hbm.at[:, wide(pair, 1)], grad.at[pair, 1], load_sem.at[8 + pair, 1]),
        ])
    for pair in range(8):
        loads.append([
            pltpu.make_async_copy(wdn_hbm.at[:, pl.ds(pair * 768, 768)], wdn.at[pair], load_sem.at[16 + pair, 0]),
        ])

    def begin(group):
        for copy in loads[group]:
            copy.start()

    def finish(group):
        for copy in loads[group]:
            copy.wait()

    sent = []

    def send(source, target, sem, to):
        copy = pltpu.make_async_remote_copy(
            src_ref=source, dst_ref=target, send_sem=out_sem.at[sem], recv_sem=in_sem.at[sem],
            device_id=to, device_id_type=MESH,
        )
        copy.start()
        sent.append(copy)
        return copy

    def to_mate(source, target, sem):
        copy = pltpu.make_async_remote_copy(
            src_ref=source, dst_ref=target, send_sem=mate_send.at[sem], recv_sem=mate_recv.at[sem],
            device_id=mate, device_id_type=MESH,
        )
        copy.start()
        sent.append(copy)
        return copy

    for group in range(AHEAD):
        begin(group)
    mate_grad = []
    for pair in range(8):
        finish(pair)
        begin(pair + AHEAD)
        block = jnp.concatenate([tok[pair, 0], tok[pair, 1]], axis=1)
        piece = jnp.dot(block, wup[pair], preferred_element_type=F32)
        pre[...] = piece if pair == 0 else pre[...] + piece
        if pair == 1:
            pl.semaphore_wait(barrier, 10)
            for other in range(8):
                mate_grad.append(to_mate(grad_hbm.at[:, wide(other, 1 - core)], grad_mate.at[other], other))
    for group in range(8 + AHEAD, 24):
        begin(group)
    mate_tok = to_mate(tok.at[:, 1 - core], tok_mate, 8)

    def put_turned(target, i, value):
        target[:, :, pl.ds(pl.multiple_of(i * 128, 128), 128)] = value.astype(BF16).T.reshape(8, 64, 128)

    @pl.loop(0, 4)
    def _(i):
        p = pre[pl.ds(pl.multiple_of(i * 128, 128), 128), :]
        put_turned(act, i, p * (0.5 * (1.0 + lax.erf(p / ROOT2))))

    mate_act = to_mate(act, act_mate, 9)

    def term(left, left_mate, right, right_mate, color, shifts):
        first = orders[color][0]
        lanes = pl.ds(color * 128, 128)
        places = [remainder(at[first] + shift, 4) for shift in shifts]
        if color == 0:
            (place,) = places
            pairs = [(place // 2) * 4 + z for z in range(4)]
            rows = [pl.ds(remainder(place, 2) * 4, 4)]
        elif color == 1:
            pairs = list(range(8))
            rows = [pl.ds(lo * 4 + place, 1) for place in places for lo in range(2)]
        else:
            (place,) = places
            pairs = [place, 4 + place]
            rows = [pl.ds(0, 8)]

        def lhs(ref):
            return jnp.concatenate([ref[r].reshape(r.size * 64, TOK) for r in rows], axis=0)

        a = jnp.concatenate([lhs(left), lhs(left_mate)], axis=1)
        b = jnp.concatenate([
            jnp.concatenate([right[p, core, :, lanes] for p in pairs], axis=1),
            jnp.concatenate([right_mate[p, :, lanes] for p in pairs], axis=1),
        ], axis=0)
        out = jnp.dot(a, b, preferred_element_type=F32)
        chunks = []
        for i in range(len(shifts)):
            got = {}
            for second in range(4):
                for third in range(4):
                    if color == 0:
                        r, l = second * 64, third * 128
                    elif color == 1:
                        r, l = i * 128 + (third % 2) * 64, ((third // 2) * 4 + second) * 128
                    else:
                        r, l = ((second % 2) * 4 + third) * 64, (second // 2) * 128
                    got[second * 4 + third] = out[r:r + 64, l:l + 128]
            chunks.append(got)
        return chunks

    operands = {DOWN: (act, act_mate, grad, grad_mate), UP: (hid, hid_mate, tok, tok_mate)}
    pend = {}

    def keep(bucket, color, shift, chunk):
        for i, value in chunk.items():
            if shift == 0:
                own1[bucket, color, i] = value
            else:
                part[bucket, color, shift - 1, i] = value.astype(BF16)

    def sem_at(bucket, color, which):
        return (bucket * 3 + color) * 15 + which

    def start_far(bucket, color):
        (chunk,) = term(*operands[bucket], color, (2,))
        keep(bucket, color, 2, chunk)
        axis = orders[color][0]
        u = (bucket, color)
        pend[u, 0] = send(part.at[bucket, color, 1, pl.ds(0, 8)], far1.at[bucket, color, 0], sem_at(*u, 0), peer(axis, 1))
        pend[u, 1] = send(part.at[bucket, color, 1, pl.ds(8, 8)], far1.at[bucket, color, 1], sem_at(*u, 1), peer(axis, 3))

    def send_near(bucket, color, shift):
        axis = orders[color][0]
        u = (bucket, color)
        if shift == 1:
            pend[u, 2] = send(part.at[bucket, color, 0, pl.ds(8, 8)], got1.at[bucket, color, 0, pl.ds(8, 8)], sem_at(*u, 2), peer(axis, 1))
        else:
            pend[u, 3] = send(part.at[bucket, color, 2, pl.ds(0, 8)], got1.at[bucket, color, 1, pl.ds(0, 8)], sem_at(*u, 3), peer(axis, 3))

    def start_near(bucket, color):
        if color == 1:
            chunks = term(*operands[bucket], color, (1, 3, 0))
        else:
            chunks = [term(*operands[bucket], color, (shift,))[0] for shift in (1, 3)]
        keep(bucket, color, 1, chunks[0])
        send_near(bucket, color, 1)
        keep(bucket, color, 3, chunks[1])
        send_near(bucket, color, 3)
        if color == 1:
            keep(bucket, color, 0, chunks[2])

    def start_own(bucket, color):
        if color != 1:
            keep(bucket, color, 0, term(*operands[bucket], color, (0,))[0])

    def merge1(bucket, color):
        axis = orders[color][0]
        u = (bucket, color)
        pend[u, 0].wait_recv()
        low, high = pl.ds(0, 8), pl.ds(8, 8)
        part[bucket, color, 0, low] = (
            part[bucket, color, 0, low].astype(F32) + far1[bucket, color, 0].astype(F32)
        ).astype(BF16)
        pend[u, 4] = send(part.at[bucket, color, 0, low], got1.at[bucket, color, 0, low], sem_at(*u, 4), peer(axis, 1))
        pend[u, 1].wait_recv()
        part[bucket, color, 2, high] = (
            part[bucket, color, 2, high].astype(F32) + far1[bucket, color, 1].astype(F32)
        ).astype(BF16)
        pend[u, 5] = send(part.at[bucket, color, 2, high], got1.at[bucket, color, 1, high], sem_at(*u, 5), peer(axis, 3))

    def finish1(bucket, color):
        axis = orders[color][1]
        u = (bucket, color)
        for which in (2, 3, 4, 5):
            pend[u, which].wait_recv()

        def total(shift):
            place = pl.ds(remainder(at[axis] + shift, 4) * 4, 4)
            return (
                own1[bucket, color, place]
                + got1[bucket, color, 0, place].astype(F32)
                + got1[bucket, color, 1, place].astype(F32)
            )

        send2[bucket, color, 1] = total(2).astype(BF16)
        pend[u, 6] = send(send2.at[bucket, color, 1, pl.ds(0, 2)], far2.at[bucket, color, 0], sem_at(*u, 6), peer(axis, 1))
        pend[u, 7] = send(send2.at[bucket, color, 1, pl.ds(2, 2)], far2.at[bucket, color, 1], sem_at(*u, 7), peer(axis, 3))
        send2[bucket, color, 0] = total(1).astype(BF16)
        pend[u, 8] = send(send2.at[bucket, color, 0, pl.ds(2, 2)], got2.at[bucket, color, 0, pl.ds(2, 2)], sem_at(*u, 8), peer(axis, 1))
        send2[bucket, color, 2] = total(3).astype(BF16)
        pend[u, 9] = send(send2.at[bucket, color, 2, pl.ds(0, 2)], got2.at[bucket, color, 1, pl.ds(0, 2)], sem_at(*u, 9), peer(axis, 3))
        own2[bucket, color] = total(0)

    def merge2(bucket, color):
        axis = orders[color][1]
        u = (bucket, color)
        pend[u, 6].wait_recv()
        low, high = pl.ds(0, 2), pl.ds(2, 2)
        send2[bucket, color, 0, low] = (
            send2[bucket, color, 0, low].astype(F32) + far2[bucket, color, 0].astype(F32)
        ).astype(BF16)
        pend[u, 10] = send(send2.at[bucket, color, 0, low], got2.at[bucket, color, 0, low], sem_at(*u, 10), peer(axis, 1))
        pend[u, 7].wait_recv()
        send2[bucket, color, 2, high] = (
            send2[bucket, color, 2, high].astype(F32) + far2[bucket, color, 1].astype(F32)
        ).astype(BF16)
        pend[u, 11] = send(send2.at[bucket, color, 2, high], got2.at[bucket, color, 1, high], sem_at(*u, 11), peer(axis, 3))

    def finish2(bucket, color):
        axis = orders[color][2]
        u = (bucket, color)
        for which in (8, 9, 10, 11):
            pend[u, which].wait_recv()
        for shift in (2, 1, 3):
            place = remainder(at[axis] + shift, 4)
            send3[bucket, color, shift - 1] = (
                own2[bucket, color, place]
                + got2[bucket, color, 0, place].astype(F32)
                + got2[bucket, color, 1, place].astype(F32)
            ).astype(BF16)
            pend[u, 11 + shift] = send(
                send3.at[bucket, color, shift - 1], got3.at[bucket, color, shift - 1], sem_at(*u, 11 + shift), peer(axis, shift)
            )

    def finish3(bucket, color):
        axis = orders[color][2]
        u = (bucket, color)
        place = at[axis]
        total = (
            own2[bucket, color, place]
            + got2[bucket, color, 0, place].astype(F32)
            + got2[bucket, color, 1, place].astype(F32)
        )
        for shift in (1, 3, 2):
            pend[u, 11 + shift].wait_recv()
            total = total + got3[bucket, color, shift - 1].astype(F32)
        out = dn_ref if bucket == DOWN else up_ref
        out[:, pl.ds(color * 128, 128)] = total * factor

    colors = (0, 2, 1)

    for pair in range(8):
        finish(8 + pair)
        mate_grad[pair].wait_recv()
    mate_act.wait_recv()
    for color in colors:
        start_far(DOWN, color)
    for color in colors:
        start_near(DOWN, color)
    for color in colors:
        start_own(DOWN, color)

    def linear(pair):
        finish(16 + pair)
        block = jnp.concatenate([grad[pair, 0], grad[pair, 1]], axis=1)
        piece = lax.dot_general(block, wdn[pair], (((1,), (1,)), ((), ())), preferred_element_type=F32)
        lin[...] = piece if pair == 0 else lin[...] + piece

    for pair in range(4):
        linear(pair)
    for color in colors:
        merge1(DOWN, color)
    for pair in range(4, 8):
        linear(pair)

    @pl.loop(0, 4)
    def _(i):
        rows = pl.ds(pl.multiple_of(i * 128, 128), 128)
        p = pre[rows, :]
        slope = 0.5 * (1.0 + lax.erf(p / ROOT2)) + p * (jnp.exp(-0.5 * p * p) / ROOT2PI)
        put_turned(hid, i, lin[rows, :] * slope)

    mate_hid = to_mate(hid, hid_mate, 10)
    mate_tok.wait_recv()
    mate_hid.wait_recv()
    for color in colors:
        start_far(UP, color)
    for color in colors:
        start_near(UP, color)
    for color in colors:
        finish1(DOWN, color)
    for color in colors:
        start_own(UP, color)
    for color in colors:
        merge2(DOWN, color)
    for color in colors:
        merge1(UP, color)
    for color in colors:
        finish2(DOWN, color)
    for color in colors:
        finish3(DOWN, color)
    for color in colors:
        finish1(UP, color)
    for color in colors:
        merge2(UP, color)
    for color in colors:
        finish2(UP, color)
    for color in colors:
        finish3(UP, color)
    for copy in sent:
        copy.wait_send()


def local(tokens, grad_out, w_up, w_down):
    total_tokens = tokens.shape[0] * lax.axis_size("row") * lax.axis_size("col")
    factor = 1.0 / math.sqrt(total_tokens)
    anywhere = pl.BlockSpec(memory_space=pl.ANY)
    inside = pl.BlockSpec(memory_space=pltpu.VMEM)
    shape = jax.ShapeDtypeStruct((64, 384), F32)
    up, down = pl.pallas_call(
        functools.partial(kernel, factor),
        out_shape=(shape, shape),
        in_specs=[anywhere] * 4,
        out_specs=(inside, inside),
        scratch_shapes=[
            pltpu.VMEM((8, 2, TOK, 384), BF16),
            pltpu.VMEM((8, 2, TOK, 384), BF16),
            pltpu.VMEM((8, 768, HID), BF16),
            pltpu.VMEM((8, HID, 768), BF16),
            pltpu.VMEM((8, TOK, 384), BF16),
            pltpu.VMEM((8, TOK, 384), BF16),
            pltpu.VMEM((TOK, HID), F32),
            pltpu.VMEM((TOK, HID), F32),
            pltpu.VMEM((8, 64, TOK), BF16),
            pltpu.VMEM((8, 64, TOK), BF16),
            pltpu.VMEM((8, 64, TOK), BF16),
            pltpu.VMEM((8, 64, TOK), BF16),
            pltpu.VMEM((2, 3, 3, 16, 64, 128), BF16),
            pltpu.VMEM((2, 3, 16, 64, 128), F32),
            pltpu.VMEM((2, 3, 2, 8, 64, 128), BF16),
            pltpu.VMEM((2, 3, 2, 16, 64, 128), BF16),
            pltpu.VMEM((2, 3, 3, 4, 64, 128), BF16),
            pltpu.VMEM((2, 3, 4, 64, 128), F32),
            pltpu.VMEM((2, 3, 2, 2, 64, 128), BF16),
            pltpu.VMEM((2, 3, 2, 4, 64, 128), BF16),
            pltpu.VMEM((2, 3, 3, 64, 128), BF16),
            pltpu.VMEM((2, 3, 3, 64, 128), BF16),
            pltpu.SemaphoreType.DMA((24, 3)),
            pltpu.SemaphoreType.DMA((11,)),
            pltpu.SemaphoreType.DMA((11,)),
            pltpu.SemaphoreType.DMA((90,)),
            pltpu.SemaphoreType.DMA((90,)),
        ],
        compiler_params=pltpu.CompilerParams(
            collective_id=0, has_side_effects=True, vmem_limit_bytes=66_000_000
        ),
    )(tokens, grad_out, w_up, w_down)
    return up.T, down.T


def solution(mesh):
    placed = (P(("row", "col"), None), P(("row", "col"), None), P(), P())
    return jax.shard_map(
        local,
        mesh=mesh,
        in_specs=placed,
        out_specs=(P("row", "col"), P("row", "col")),
        check_vma=False,
    )
```

time: 202 us -> 71.5 us (0.35)
  the two profiles are of different devices: /device:TPU:17 before, /device:TPU:0 now
where the time goes in v1:
time: 71.5 us; the launch traced here: 71.3 us
  Pallas kernels  67.6 us (95%)
  local copies, waits for them, and re-layouts  3.08 us (4%)
    pallas_call x1, Pallas kernels, local(): pl.pallas_call(functools.partial(kernel, factor), out_shape=(shape, shape...  67.6 us
    unnamed x2, local copies, waits for them, and re-layouts  3.08 us

profile of v1, /device:TPU:0, one launch (start us, length us, event | category | flops | bytes accessed | tf_op | source)
XLA Modules:
  0.0 71.3 jit_solution(12140643868033502850)
XLA Ops:
  0.6 67.6 %shard_map.59 = (f32[64,384]{1,0:T(8,128)}, f32[64,384]{1,0:T(8,128)}) custom-call(bf16[512,6144]{1,0:T(8,128)(2,1)} %tok_hbm.1, bf16[512,6144]{1,0:T(8,128)(2,1)} %grad_hbm.1, bf16[6144,512]{1,0:T(8,128)(2,1)} %wup_hbm.1, bf16[512,6144]{1,0:T(8,128)(2,1)} %wdn_hbm.1), custom_call_target="tpu_custom_call" | custom-call | tf_op jit(solution)/shard_map/pallas_call | solution.py:368
  68.2 1.5 %copy.8 = f32[384,64]{0,1:T(8,128)} copy(f32[384,64]{0,1:T(8,128)} %bitcast.3) | data formatting | bytes 196608
  69.8 1.5 %copy.9 = f32[384,64]{0,1:T(8,128)} copy(f32[384,64]{0,1:T(8,128)} %bitcast.2) | data formatting | bytes 196608

commit v2 on v1

v2 whole, which is shorter than its diff:
```python
import math

import jax
import jax.numpy as jnp
from jax import lax
from jax.experimental import pallas as pl
from jax.experimental.pallas import tpu as pltpu
from jax.sharding import PartitionSpec as P

MESH = pl.DeviceIdType.MESH
BF16, F32 = jnp.bfloat16, jnp.float32
ROOT2, ROOT2PI = math.sqrt(2.0), math.sqrt(2.0 * math.pi)
DOWN, UP = 0, 1
TOK, WIDTH, HID = 512, 6144, 512
AHEAD = 3
EARLY = 2


def remainder(a, n):
    return lax.rem(a, jnp.int32(n))


def kernel(
    tok_hbm, grad_hbm, wup_hbm, wdn_hbm,
    up_ref, dn_ref,
    tok, grad, wup, wdn, tok_mate, grad_mate,
    pre, lin, act, act_mate, hid, hid_mate,
    part, own1, far1, got1, send2, own2, got2, send3, own3, got3,
    load_sem, mate_send, mate_recv, out_sem, in_sem,
):
    row, col = lax.axis_index("row"), lax.axis_index("col")
    core = remainder(row, 2)
    at = {
        "x": (row // 8) * 2 + col // 4,
        "y": remainder(col, 4),
        "z": remainder(row // 2, 4),
    }
    mate = (row + 1 - 2 * core, col)

    def peer(axis, shift):
        to = dict(at)
        to[axis] = remainder(at[axis] + shift, 4)
        return ((to["x"] // 2) * 8 + to["z"] * 2 + core, remainder(to["x"], 2) * 4 + to["y"])

    orders = (("x", "y", "z"), ("y", "z", "x"), ("z", "x", "y"))

    barrier = pltpu.get_barrier_semaphore()
    pl.semaphore_signal(barrier, inc=1, device_id=mate, device_id_type=MESH)
    for axis in ("x", "y", "z"):
        for shift in (1, 3, 2):
            pl.semaphore_signal(barrier, inc=1, device_id=peer(axis, shift), device_id_type=MESH)

    top, deep = at["x"] // 2, at["z"]
    places = [(1 - top, 2), (top, 2), (1 - top, 0), (1 - top, 1), (1 - top, 3), (top, 0), (top, 1), (top, 3)]
    needed = [h * 4 + remainder(deep + d, 4) for h, d in places]

    def both(pair):
        return pl.ds(pl.multiple_of(pair * 768, 128), 768)

    def wide(pair, half):
        return pl.ds(pl.multiple_of(pair * 768 + half * 384, 128), 384)

    loads = []
    for pair in range(8):
        loads.append([
            pltpu.make_async_copy(wup_hbm.at[pl.ds(pair * 768, 768), :], wup.at[pair], load_sem.at[pair]),
            pltpu.make_async_copy(tok_hbm.at[:, wide(pair, 0)], tok.at[pair, 0], load_sem.at[8 + pair]),
            pltpu.make_async_copy(tok_hbm.at[:, wide(pair, 1)], tok.at[pair, 1], load_sem.at[8 + pair]),
        ])
    grad_loads = [[
        pltpu.make_async_copy(grad_hbm.at[:, wide(pair, 0)], grad.at[pair, 0], load_sem.at[16 + i]),
        pltpu.make_async_copy(grad_hbm.at[:, wide(pair, 1)], grad.at[pair, 1], load_sem.at[16 + i]),
    ] for i, pair in enumerate(needed)]
    wdn_loads = [[
        pltpu.make_async_copy(wdn_hbm.at[:, both(pair)], wdn.at[pair], load_sem.at[24 + i]),
    ] for i, pair in enumerate(needed)]
    for i in range(EARLY):
        loads += [grad_loads[i], wdn_loads[i]]
    loads += grad_loads[EARLY:] + wdn_loads[EARLY:]

    def begin(group):
        for copy in loads[group]:
            copy.start()

    def finish(ref, sem):
        pltpu.make_async_copy(ref, ref, load_sem.at[sem]).wait()

    sent = []

    def send(source, target, phase, sem, to):
        pltpu.make_async_remote_copy(
            src_ref=source, dst_ref=target, send_sem=out_sem.at[phase], recv_sem=in_sem.at[sem],
            device_id=to, device_id_type=MESH,
        ).start()

    def sem_at(bucket, color, which):
        return (bucket * 3 + color) * 5 + which

    def arrived(ref, bucket, color, which):
        pltpu.make_async_copy(ref, ref, in_sem.at[sem_at(bucket, color, which)]).wait()

    def to_mate(source, target, sem):
        copy = pltpu.make_async_remote_copy(
            src_ref=source, dst_ref=target, send_sem=mate_send.at[sem], recv_sem=mate_recv.at[sem],
            device_id=mate, device_id_type=MESH,
        )
        copy.start()
        sent.append(copy)
        return copy

    mate_grad = []

    def offer(i):
        mate_grad.append(to_mate(grad_hbm.at[:, wide(needed[i], 1 - core)], grad_mate.at[needed[i]], i))

    for group in range(AHEAD):
        begin(group)
    with jax.named_scope("barrier"):
        pl.semaphore_wait(barrier, 10)
    for pair in range(8):
        with jax.named_scope(f"preact{pair}"):
            finish(wup.at[pair], pair)
            finish(tok.at[pair], 8 + pair)
            begin(pair + AHEAD)
            if pair < 6:
                offer(pair)
            block = jnp.concatenate([tok[pair, 0], tok[pair, 1]], axis=1)
            piece = jnp.dot(block, wup[pair], preferred_element_type=F32)
            pre[...] = piece if pair == 0 else pre[...] + piece
    for group in range(8 + AHEAD, 16 + EARLY):
        begin(group)

    def put_turned(target, i, value):
        target[:, :, pl.ds(pl.multiple_of(i * 128, 128), 128)] = value.astype(BF16).T.reshape(8, 64, 128)

    with jax.named_scope("turn_act"):
        @pl.loop(0, 4)
        def _(i):
            p = pre[pl.ds(pl.multiple_of(i * 128, 128), 128), :]
            put_turned(act, i, p * (0.5 * (1.0 + lax.erf(p / ROOT2))))

    mate_act = to_mate(act, act_mate, 9)
    offer(6)
    offer(7)
    mate_tok = to_mate(tok.at[:, 1 - core], tok_mate, 8)

    def term(left, left_mate, right, right_mate, color, shifts):
        first = orders[color][0]
        lanes = pl.ds(color * 128, 128)
        places = [remainder(at[first] + shift, 4) for shift in shifts]
        if color == 0:
            (place,) = places
            pairs = [(place // 2) * 4 + z for z in range(4)]
            rows = [pl.ds(remainder(place, 2) * 4, 4)]
        elif color == 1:
            pairs = list(range(8))
            rows = [pl.ds(lo * 4 + place, 1) for place in places for lo in range(2)]
        else:
            (place,) = places
            pairs = [place, 4 + place]
            rows = [pl.ds(0, 8)]

        def lhs(ref):
            return jnp.concatenate([ref[r].reshape(r.size * 64, TOK) for r in rows], axis=0)

        a = jnp.concatenate([lhs(left), lhs(left_mate)], axis=1)
        b = jnp.concatenate([
            jnp.concatenate([right[p, core, :, lanes] for p in pairs], axis=1),
            jnp.concatenate([right_mate[p, :, lanes] for p in pairs], axis=1),
        ], axis=0)
        out = jnp.dot(a, b, preferred_element_type=F32)
        chunks = []
        for i in range(len(shifts)):
            got = {}
            for second in range(4):
                for third in range(4):
                    if color == 0:
                        r, l = second * 64, third * 128
                    elif color == 1:
                        r, l = i * 128 + (third % 2) * 64, ((third // 2) * 4 + second) * 128
                    else:
                        r, l = ((second % 2) * 4 + third) * 64, (second // 2) * 128
                    got[second * 4 + third] = out[r:r + 64, l:l + 128]
            chunks.append(got)
        return chunks

    operands = {DOWN: (act, act_mate, grad, grad_mate), UP: (hid, hid_mate, tok, tok_mate)}
    pend = {}
    low, high = pl.ds(0, 8), pl.ds(8, 8)

    def keep(bucket, color, shift, chunk):
        for i, value in chunk.items():
            if shift == 0:
                own1[bucket, color, i] = value
            else:
                part[bucket, color, shift - 1, i] = value.astype(BF16)

    def start_far(bucket, *colors):
        chunks = [term(*operands[bucket], color, (2,))[0] for color in colors]
        for color, chunk in zip(colors, chunks):
            keep(bucket, color, 2, chunk)
        for color in colors:
            axis = orders[color][0]
            send(part.at[bucket, color, 1, low], far1.at[bucket, color, 0], 0, sem_at(bucket, color, 0), peer(axis, 1))
            send(part.at[bucket, color, 1, high], far1.at[bucket, color, 1], 0, sem_at(bucket, color, 1), peer(axis, 3))

    def send_next(bucket, color, half):
        send(part.at[bucket, color, 0, half], got1.at[bucket, color, 0, half], 0, sem_at(bucket, color, 2), peer(orders[color][0], 1))

    def send_last(bucket, color, half):
        send(part.at[bucket, color, 2, half], got1.at[bucket, color, 1, half], 0, sem_at(bucket, color, 2), peer(orders[color][0], 3))

    def start_near(bucket, color):
        if color == 1:
            chunks = term(*operands[bucket], color, (1, 3, 0))
        else:
            chunks = [term(*operands[bucket], color, (shift,))[0] for shift in (1, 3)]
        keep(bucket, color, 1, chunks[0])
        send_next(bucket, color, high)
        keep(bucket, color, 3, chunks[1])
        send_last(bucket, color, low)
        if color == 1:
            keep(bucket, color, 0, chunks[2])

    def start_own(bucket, *colors):
        chunks = [term(*operands[bucket], color, (0,))[0] for color in colors]
        for color, chunk in zip(colors, chunks):
            keep(bucket, color, 0, chunk)

    def merge1(bucket, color):
        for side, shift, half, forward in ((0, 1, low, send_next), (1, 3, high, send_last)):
            arrived(far1.at[bucket, color, side], bucket, color, side)
            part[bucket, color, shift - 1, half] = (
                part[bucket, color, shift - 1, half].astype(F32) + far1[bucket, color, side].astype(F32)
            ).astype(BF16)
            forward(bucket, color, half)

    def finish1(bucket, color):
        axis = orders[color][1]
        arrived(got1.at[bucket, color], bucket, color, 2)

        def total(shift):
            place = pl.ds(remainder(at[axis] + shift, 4) * 4, 4)
            return (
                own1[bucket, color, place]
                + got1[bucket, color, 0, place].astype(F32)
                + got1[bucket, color, 1, place].astype(F32)
            )

        for shift in (2, 1, 3):
            send2[bucket, color, shift - 1] = total(shift).astype(BF16)
            send(send2.at[bucket, color, shift - 1], got2.at[bucket, color, shift - 1], 1, sem_at(bucket, color, 3), peer(axis, shift))
        own2[bucket, color] = total(0)

    def finish2(bucket, color):
        axis = orders[color][2]
        arrived(got2.at[bucket, color], bucket, color, 3)

        def total(place):
            value = own2[bucket, color, place]
            for i in range(3):
                value = value + got2[bucket, color, i, place].astype(F32)
            return value

        for shift in (2, 1, 3):
            send3[bucket, color, shift - 1] = total(remainder(at[axis] + shift, 4)).astype(BF16)
            send(send3.at[bucket, color, shift - 1], got3.at[bucket, color, shift - 1], 2, sem_at(bucket, color, 4), peer(axis, shift))
        own3[bucket, color] = total(at[axis])

    def finish3(bucket, color):
        arrived(got3.at[bucket, color], bucket, color, 4)
        value = own3[bucket, color]
        for i in range(3):
            value = value + got3[bucket, color, i].astype(F32)
        out = dn_ref if bucket == DOWN else up_ref
        out[:, pl.ds(color * 128, 128)] = value

    colors = (2, 0, 1)

    def linear(*order):
        for i in order:
            pair = needed[i]
            finish(wdn.at[pair], 24 + i)
            if i < EARLY:
                finish(grad.at[pair], 16 + i)
            block = jnp.concatenate([grad[pair, 0], grad[pair, 1]], axis=1)
            piece = lax.dot_general(block, wdn[pair], (((1,), (1,)), ((), ())), preferred_element_type=F32)
            lin[...] = piece if i == 0 else lin[...] + piece

    def ready_down(*order):
        for i in order:
            if i >= EARLY:
                finish(grad.at[needed[i]], 16 + i)
            mate_grad[i].wait_recv()

    def ready_act():
        mate_act.wait_recv()
        for group in range(16 + EARLY, 24):
            begin(group)

    def turn_hid():
        @pl.loop(0, 4)
        def _(i):
            rows = pl.ds(pl.multiple_of(i * 128, 128), 128)
            p = pre[rows, :]
            slope = 0.5 * (1.0 + lax.erf(p / ROOT2)) + p * (jnp.exp(-0.5 * p * p) / ROOT2PI)
            put_turned(hid, i, lin[rows, :] * slope)

        pend["hid"] = to_mate(hid, hid_mate, 10)

    def ready_up():
        mate_tok.wait_recv()
        pend["hid"].wait_recv()

    def drain():
        for copy in sent:
            copy.wait_send()
        for phase, ref in enumerate((part, send2, send3)):
            pltpu.make_async_copy(ref, ref, out_sem.at[phase]).wait()

    def one(step, bucket, *colors):
        with jax.named_scope(f"{step.__name__}_{'DU'[bucket]}" + "".join(map(str, colors))):
            step(bucket, *colors)

    def each(step, bucket):
        for color in colors:
            one(step, bucket, color)

    def alone(step, *args):
        with jax.named_scope(step.__name__ + "_".join(str(a) for a in args)):
            step(*args)

    for i in range(EARLY):
        alone(linear, i)
    alone(ready_act)
    alone(ready_down, 0, 1, 2, 3, 4)
    one(start_far, DOWN, 2, 0)
    alone(ready_down, 5, 6, 7)
    one(start_far, DOWN, 1)
    each(start_near, DOWN)
    alone(linear, 2, 3, 4, 5, 6, 7)
    each(merge1, DOWN)
    alone(turn_hid)
    one(start_own, DOWN, 2, 0)
    alone(ready_up)
    one(start_far, UP, 2, 0)
    one(start_far, UP, 1)
    each(finish1, DOWN)
    each(start_near, UP)
    one(start_own, UP, 2, 0)
    each(merge1, UP)
    each(finish2, DOWN)
    each(finish1, UP)
    each(finish3, DOWN)
    each(finish2, UP)
    each(finish3, UP)
    alone(drain)


def local(tokens, grad_out, w_up, w_down):
    total_tokens = tokens.shape[0] * lax.axis_size("row") * lax.axis_size("col")
    factor = 1.0 / math.sqrt(total_tokens)
    anywhere = pl.BlockSpec(memory_space=pl.ANY)
    inside = pl.BlockSpec(memory_space=pltpu.VMEM)
    shape = pltpu.VMEM((64, 384), F32)
    up, down = pl.pallas_call(
        kernel,
        out_shape=(shape, shape),
        in_specs=[anywhere] * 4,
        out_specs=(inside, inside),
        scratch_shapes=[
            pltpu.VMEM((8, 2, TOK, 384), BF16),
            pltpu.VMEM((8, 2, TOK, 384), BF16),
            pltpu.VMEM((8, 768, HID), BF16),
            pltpu.VMEM((8, HID, 768), BF16),
            pltpu.VMEM((8, TOK, 384), BF16),
            pltpu.VMEM((8, TOK, 384), BF16),
            pltpu.VMEM((TOK, HID), F32),
            pltpu.VMEM((TOK, HID), F32),
            pltpu.VMEM((8, 64, TOK), BF16),
            pltpu.VMEM((8, 64, TOK), BF16),
            pltpu.VMEM((8, 64, TOK), BF16),
            pltpu.VMEM((8, 64, TOK), BF16),
            pltpu.VMEM((2, 3, 3, 16, 64, 128), BF16),
            pltpu.VMEM((2, 3, 16, 64, 128), F32),
            pltpu.VMEM((2, 3, 2, 8, 64, 128), BF16),
            pltpu.VMEM((2, 3, 2, 16, 64, 128), BF16),
            pltpu.VMEM((2, 3, 3, 4, 64, 128), BF16),
            pltpu.VMEM((2, 3, 4, 64, 128), F32),
            pltpu.VMEM((2, 3, 3, 4, 64, 128), BF16),
            pltpu.VMEM((2, 3, 3, 64, 128), BF16),
            pltpu.VMEM((2, 3, 64, 128), F32),
            pltpu.VMEM((2, 3, 3, 64, 128), BF16),
            pltpu.SemaphoreType.DMA((32,)),
            pltpu.SemaphoreType.DMA((11,)),
            pltpu.SemaphoreType.DMA((11,)),
            pltpu.SemaphoreType.DMA((3,)),
            pltpu.SemaphoreType.DMA((30,)),
        ],
        compiler_params=pltpu.CompilerParams(
            collective_id=0, has_side_effects=True, vmem_limit_bytes=66_000_000
        ),
    )(tokens, grad_out, w_up, w_down)
    return up.T * factor, down.T * factor


def solution(mesh):
    placed = (P(("row", "col"), None), P(("row", "col"), None), P(), P())
    return jax.shard_map(
        local,
        mesh=mesh,
        in_specs=placed,
        out_specs=(P("row", "col"), P("row", "col")),
        check_vma=False,
    )
```

time: 71.5 us -> 48.5 us (0.68)
  Pallas kernels: 67.6 us -> 46.9 us
  local copies, waits for them, and re-layouts: 3.08 us -> 0 us
    pallas_call x1, Pallas kernels: 67.6 us -> 46.9 us  [local(): pl.pallas_call(kernel, out_shape=(shape, shape), in_specs=[anywhere] * 4,...]
    unnamed x2 -> x0, local copies, waits for them, and re-layouts: 3.08 us -> none
where the time goes in v2:
time: 48.5 us; the launch traced here: 48.2 us
  Pallas kernels  46.9 us (97%)
  other arithmetic  0.69 us (1%)
  between operations  0.64 us (1%)
    pallas_call x1, Pallas kernels, local(): pl.pallas_call(kernel, out_shape=(shape, shape), in_specs=[anywhere] * 4,...  46.9 us

profile of v2, /device:TPU:0, one launch (start us, length us, event | category | flops | bytes accessed | tf_op | source)
XLA Modules:
  0.0 48.2 jit_solution(8931445661405035460)
XLA Ops:
  0.6 46.9 %shard_map.59 = (f32[64,384]{1,0:T(8,128)S(1)}, f32[64,384]{1,0:T(8,128)S(1)}) custom-call(bf16[512,6144]{1,0:T(8,128)(2,1)} %tok_hbm.1, bf16[512,6144]{1,0:T(8,128)(2,1)} %grad_hbm.1, bf16[6144,512]{1,0:T(8,128)(2,1)} %wup_hbm.1, bf16[512,6144]{1,0:T(8,128)(2,1)} %wdn_hbm.1), custom_call_target="tpu_custom_call" | custom-call | tf_op jit(solution)/shard_map/pallas_call | solution.py:366
  47.5 0.7 %multiply_bitcast_fusion = (f32[384,64]{0,1:T(8,128)}, f32[384,64]{0,1:T(8,128)}) fusion(f32[64,384]{1,0:T(8,128)S(1)} %get-tuple-element.5, f32[64,384]{1,0:T(8,128)S(1)} %get-tuple-element.4), kind=kLoop, calls=%fused_computation | loop fusion | flops 49152 | bytes 393216 | tf_op jit(solution)/shard_map/mul | solution.py:404

commit v3 on v2

--- a/solution.py
+++ b/solution.py
@@ -12,8 +12,7 @@
 ROOT2, ROOT2PI = math.sqrt(2.0), math.sqrt(2.0 * math.pi)
 DOWN, UP = 0, 1
 TOK, WIDTH, HID = 512, 6144, 512
-AHEAD = 3
-EARLY = 2
+AHEAD = 4
 
 
 def remainder(a, n):
@@ -67,16 +66,14 @@
             pltpu.make_async_copy(tok_hbm.at[:, wide(pair, 0)], tok.at[pair, 0], load_sem.at[8 + pair]),
             pltpu.make_async_copy(tok_hbm.at[:, wide(pair, 1)], tok.at[pair, 1], load_sem.at[8 + pair]),
         ])
-    grad_loads = [[
-        pltpu.make_async_copy(grad_hbm.at[:, wide(pair, 0)], grad.at[pair, 0], load_sem.at[16 + i]),
-        pltpu.make_async_copy(grad_hbm.at[:, wide(pair, 1)], grad.at[pair, 1], load_sem.at[16 + i]),
-    ] for i, pair in enumerate(needed)]
-    wdn_loads = [[
-        pltpu.make_async_copy(wdn_hbm.at[:, both(pair)], wdn.at[pair], load_sem.at[24 + i]),
-    ] for i, pair in enumerate(needed)]
-    for i in range(EARLY):
-        loads += [grad_loads[i], wdn_loads[i]]
-    loads += grad_loads[EARLY:] + wdn_loads[EARLY:]
+    own_loads, other_loads, wdn_loads = [], [], []
+    for i, pair in enumerate(needed):
+        own_loads.append([pltpu.make_async_copy(grad_hbm.at[:, wide(pair, core)], grad.at[pair, core], load_sem.at[16 + i])])
+        other_loads.append([pltpu.make_async_copy(grad_hbm.at[:, wide(pair, 1 - core)], grad.at[pair, 1 - core], load_sem.at[24 + i])])
+        wdn_loads.append([pltpu.make_async_copy(wdn_hbm.at[:, both(pair)], wdn.at[pair], load_sem.at[32 + i])])
+    loads += own_loads
+    for i in range(8):
+        loads.append(other_loads[i] + wdn_loads[i])
 
     def begin(group):
         for copy in loads[group]:
@@ -127,24 +124,34 @@
             block = jnp.concatenate([tok[pair, 0], tok[pair, 1]], axis=1)
             piece = jnp.dot(block, wup[pair], preferred_element_type=F32)
             pre[...] = piece if pair == 0 else pre[...] + piece
-    for group in range(8 + AHEAD, 16 + EARLY):
+    for group in range(8 + AHEAD, 18):
         begin(group)
 
     def put_turned(target, i, value):
         target[:, :, pl.ds(pl.multiple_of(i * 128, 128), 128)] = value.astype(BF16).T.reshape(8, 64, 128)
 
+    def halves(source, target, sem, turn):
+        copies = []
+        for half in range(2):
+            @pl.loop(2 * half, 2 * half + 2)
+            def _(i):
+                turn(i)
+
+            lanes = pl.ds(half * 256, 256)
+            copies.append(to_mate(source.at[:, :, lanes], target.at[:, :, lanes], sem + half))
+        return copies
+
+    def turn_act(i):
+        p = pre[pl.ds(pl.multiple_of(i * 128, 128), 128), :]
+        put_turned(act, i, p * (0.5 * (1.0 + lax.erf(p / ROOT2))))
+
     with jax.named_scope("turn_act"):
-        @pl.loop(0, 4)
-        def _(i):
-            p = pre[pl.ds(pl.multiple_of(i * 128, 128), 128), :]
-            put_turned(act, i, p * (0.5 * (1.0 + lax.erf(p / ROOT2))))
-
-    mate_act = to_mate(act, act_mate, 9)
+        mate_act = halves(act, act_mate, 9, turn_act)
     offer(6)
     offer(7)
     mate_tok = to_mate(tok.at[:, 1 - core], tok_mate, 8)
 
-    def term(left, left_mate, right, right_mate, color, shifts):
+    def term(left, left_mate, right, right_mate, color, shifts, sides=("own", "mate")):
         first = orders[color][0]
         lanes = pl.ds(color * 128, 128)
         places = [remainder(at[first] + shift, 4) for shift in shifts]
@@ -163,12 +170,14 @@
         def lhs(ref):
             return jnp.concatenate([ref[r].reshape(r.size * 64, TOK) for r in rows], axis=0)
 
-        a = jnp.concatenate([lhs(left), lhs(left_mate)], axis=1)
-        b = jnp.concatenate([
-            jnp.concatenate([right[p, core, :, lanes] for p in pairs], axis=1),
-            jnp.concatenate([right_mate[p, :, lanes] for p in pairs], axis=1),
-        ], axis=0)
-        out = jnp.dot(a, b, preferred_element_type=F32)
+        a, b = [], []
+        if "own" in sides:
+            a.append(lhs(left))
+            b.append(jnp.concatenate([right[p, core, :, lanes] for p in pairs], axis=1))
+        if "mate" in sides:
+            a.append(lhs(left_mate))
+            b.append(jnp.concatenate([right_mate[p, :, lanes] for p in pairs], axis=1))
+        out = jnp.dot(jnp.concatenate(a, axis=1), jnp.concatenate(b, axis=0), preferred_element_type=F32)
         chunks = []
         for i in range(len(shifts)):
             got = {}
@@ -185,7 +194,6 @@
         return chunks
 
     operands = {DOWN: (act, act_mate, grad, grad_mate), UP: (hid, hid_mate, tok, tok_mate)}
-    pend = {}
     low, high = pl.ds(0, 8), pl.ds(8, 8)
 
     def keep(bucket, color, shift, chunk):
@@ -195,32 +203,35 @@
             else:
                 part[bucket, color, shift - 1, i] = value.astype(BF16)
 
+    def early_far(bucket, *colors):
+        chunks = [term(*operands[bucket], color, (2,), ("own",))[0] for color in colors]
+        for color, chunk in zip(colors, chunks):
+            keep(bucket, color, 0, chunk)
+
     def start_far(bucket, *colors):
-        chunks = [term(*operands[bucket], color, (2,))[0] for color in colors]
+        chunks = [term(*operands[bucket], color, (2,), ("mate",))[0] for color in colors]
         for color, chunk in zip(colors, chunks):
-            keep(bucket, color, 2, chunk)
+            keep(bucket, color, 2, {i: value + own1[bucket, color, i] for i, value in chunk.items()})
         for color in colors:
             axis = orders[color][0]
             send(part.at[bucket, color, 1, low], far1.at[bucket, color, 0], 0, sem_at(bucket, color, 0), peer(axis, 1))
             send(part.at[bucket, color, 1, high], far1.at[bucket, color, 1], 0, sem_at(bucket, color, 1), peer(axis, 3))
 
-    def send_next(bucket, color, half):
-        send(part.at[bucket, color, 0, half], got1.at[bucket, color, 0, half], 0, sem_at(bucket, color, 2), peer(orders[color][0], 1))
-
-    def send_last(bucket, color, half):
-        send(part.at[bucket, color, 2, half], got1.at[bucket, color, 1, half], 0, sem_at(bucket, color, 2), peer(orders[color][0], 3))
+    def send_next(bucket, color, half, phase=0):
+        send(part.at[bucket, color, 0, half], got1.at[bucket, color, 0, half], phase, sem_at(bucket, color, 2), peer(orders[color][0], 1))
+
+    def send_last(bucket, color, half, phase=0):
+        send(part.at[bucket, color, 2, half], got1.at[bucket, color, 1, half], phase, sem_at(bucket, color, 2), peer(orders[color][0], 3))
 
     def start_near(bucket, color):
         if color == 1:
-            chunks = term(*operands[bucket], color, (1, 3, 0))
+            chunks = term(*operands[bucket], color, (1, 3))
         else:
             chunks = [term(*operands[bucket], color, (shift,))[0] for shift in (1, 3)]
         keep(bucket, color, 1, chunks[0])
         send_next(bucket, color, high)
         keep(bucket, color, 3, chunks[1])
         send_last(bucket, color, low)
-        if color == 1:
-            keep(bucket, color, 0, chunks[2])
 
     def start_own(bucket, *colors):
         chunks = [term(*operands[bucket], color, (0,))[0] for color in colors]
@@ -233,7 +244,10 @@
             part[bucket, color, shift - 1, half] = (
                 part[bucket, color, shift - 1, half].astype(F32) + far1[bucket, color, side].astype(F32)
             ).astype(BF16)
-            forward(bucket, color, half)
+            forward(bucket, color, half, 3 + bucket * 3 + color)
+
+    def merged(bucket, color):
+        pltpu.make_async_copy(part.at[bucket, color, 0], part.at[bucket, color, 0], out_sem.at[3 + bucket * 3 + color]).wait()
 
     def finish1(bucket, color):
         axis = orders[color][1]
@@ -280,42 +294,48 @@
     def linear(*order):
         for i in order:
             pair = needed[i]
-            finish(wdn.at[pair], 24 + i)
-            if i < EARLY:
-                finish(grad.at[pair], 16 + i)
+            finish(grad.at[pair, 1 - core], 24 + i)
+            finish(wdn.at[pair], 32 + i)
             block = jnp.concatenate([grad[pair, 0], grad[pair, 1]], axis=1)
             piece = lax.dot_general(block, wdn[pair], (((1,), (1,)), ((), ())), preferred_element_type=F32)
             lin[...] = piece if i == 0 else lin[...] + piece
 
-    def ready_down(*order):
+    def ready_grad(*order):
         for i in order:
-            if i >= EARLY:
-                finish(grad.at[needed[i]], 16 + i)
+            finish(grad.at[needed[i], core], 16 + i)
+
+    def ready_mate(*order):
+        for i in order:
             mate_grad[i].wait_recv()
 
     def ready_act():
-        mate_act.wait_recv()
-        for group in range(16 + EARLY, 24):
+        for copy in mate_act:
+            copy.wait_recv()
+        for group in range(18, 24):
             begin(group)
 
-    def turn_hid():
-        @pl.loop(0, 4)
-        def _(i):
-            rows = pl.ds(pl.multiple_of(i * 128, 128), 128)
-            p = pre[rows, :]
-            slope = 0.5 * (1.0 + lax.erf(p / ROOT2)) + p * (jnp.exp(-0.5 * p * p) / ROOT2PI)
-            put_turned(hid, i, lin[rows, :] * slope)
-
-        pend["hid"] = to_mate(hid, hid_mate, 10)
+    def turn_hid(i):
+        rows = pl.ds(pl.multiple_of(i * 128, 128), 128)
+        p = pre[rows, :]
+        slope = 0.5 * (1.0 + lax.erf(p / ROOT2)) + p * (jnp.exp(-0.5 * p * p) / ROOT2PI)
+        put_turned(hid, i, lin[rows, :] * slope)
+
+    mate_hid = []
+
+    def turn_all_hid():
+        mate_hid.extend(halves(hid, hid_mate, 11, turn_hid))
 
     def ready_up():
         mate_tok.wait_recv()
-        pend["hid"].wait_recv()
+        for copy in mate_hid:
+            copy.wait_recv()
 
     def drain():
         for copy in sent:
             copy.wait_send()
-        for phase, ref in enumerate((part, send2, send3)):
+        for color in colors:
+            merged(DOWN, color)
+        for phase, ref in enumerate((part.at[:, :, pl.ds(0, 2)], send2, send3)):
             pltpu.make_async_copy(ref, ref, out_sem.at[phase]).wait()
 
     def one(step, bucket, *colors):
@@ -330,29 +350,62 @@
         with jax.named_scope(step.__name__ + "_".join(str(a) for a in args)):
             step(*args)
 
-    for i in range(EARLY):
-        alone(linear, i)
+    alone(ready_grad, 0, 1, 2, 3, 4)
+    one(early_far, DOWN, 2, 0)
+    alone(ready_grad, 5, 6, 7)
+    one(early_far, DOWN, 1)
+    alone(linear, 0)
     alone(ready_act)
-    alone(ready_down, 0, 1, 2, 3, 4)
+    alone(ready_mate, 0, 1, 2, 3, 4)
     one(start_far, DOWN, 2, 0)
-    alone(ready_down, 5, 6, 7)
+    alone(ready_mate, 5, 6, 7)
     one(start_far, DOWN, 1)
-    each(start_near, DOWN)
-    alone(linear, 2, 3, 4, 5, 6, 7)
+
+    @pl.when(core == 1)
+    def _():
+        alone(linear, 1)
+        alone(linear, 2)
+        each(start_near, DOWN)
+
+    @pl.when(core == 0)
+    def _():
+        each(start_near, DOWN)
+        alone(linear, 1)
+        alone(linear, 2)
+    alone(linear, 3)
+    alone(linear, 4)
+    alone(linear, 5)
+    alone(linear, 6)
+    alone(linear, 7)
     each(merge1, DOWN)
-    alone(turn_hid)
+    alone(turn_all_hid)
+    one(early_far, UP, 2, 0)
+    one(early_far, UP, 1)
     one(start_own, DOWN, 2, 0)
     alone(ready_up)
     one(start_far, UP, 2, 0)
     one(start_far, UP, 1)
-    each(finish1, DOWN)
-    each(start_near, UP)
-    one(start_own, UP, 2, 0)
+
+    @pl.when(core == 1)
+    def _():
+        one(start_own, DOWN, 1)
+        one(start_own, UP, 2, 0, 1)
+        each(start_near, UP)
+
+    @pl.when(core == 0)
+    def _():
+        each(start_near, UP)
+        one(start_own, DOWN, 1)
+        one(start_own, UP, 2, 0, 1)
+
     each(merge1, UP)
+    for color in colors:
+        one(merged, UP, (color + 1) % 3)
+        one(finish1, DOWN, color)
+    each(finish1, UP)
     each(finish2, DOWN)
-    each(finish1, UP)
+    each(finish2, UP)
     each(finish3, DOWN)
-    each(finish2, UP)
     each(finish3, UP)
     alone(drain)
 
@@ -391,10 +444,10 @@
             pltpu.VMEM((2, 3, 3, 64, 128), BF16),
             pltpu.VMEM((2, 3, 64, 128), F32),
             pltpu.VMEM((2, 3, 3, 64, 128), BF16),
-            pltpu.SemaphoreType.DMA((32,)),
-            pltpu.SemaphoreType.DMA((11,)),
-            pltpu.SemaphoreType.DMA((11,)),
-            pltpu.SemaphoreType.DMA((3,)),
+            pltpu.SemaphoreType.DMA((40,)),
+            pltpu.SemaphoreType.DMA((13,)),
+            pltpu.SemaphoreType.DMA((13,)),
+            pltpu.SemaphoreType.DMA((9,)),
             pltpu.SemaphoreType.DMA((30,)),
         ],
         compiler_params=pltpu.CompilerParams(

time: 48.5 us -> 46.1 us (0.951)
  Pallas kernels: 46.9 us -> 44.7 us
    pallas_call x1, Pallas kernels: 46.9 us -> 44.7 us  [local(): pl.pallas_call(kernel, out_shape=(shape, shape), in_specs=[anywhere] * 4,...]
where the time goes in v3:
time: 46.1 us; the launch traced here: 46 us
  Pallas kernels  44.7 us (97%)
  other arithmetic  0.69 us (1%)
  between operations  0.64 us (1%)
    pallas_call x1, Pallas kernels, local(): pl.pallas_call(kernel, out_shape=(shape, shape), in_specs=[anywhere] * 4,...  44.7 us

profile of v3, /device:TPU:0, one launch (start us, length us, event | category | flops | bytes accessed | tf_op | source)
XLA Modules:
  0.0 46.0 jit_solution(15883344605050400247)
XLA Ops:
  0.6 44.7 %shard_map.59 = (f32[64,384]{1,0:T(8,128)S(1)}, f32[64,384]{1,0:T(8,128)S(1)}) custom-call(bf16[512,6144]{1,0:T(8,128)(2,1)} %tok_hbm.1, bf16[512,6144]{1,0:T(8,128)(2,1)} %grad_hbm.1, bf16[6144,512]{1,0:T(8,128)(2,1)} %wup_hbm.1, bf16[512,6144]{1,0:T(8,128)(2,1)} %wdn_hbm.1), custom_call_target="tpu_custom_call" | custom-call | tf_op jit(solution)/shard_map/pallas_call | solution.py:419
  45.3 0.7 %multiply_bitcast_fusion = (f32[384,64]{0,1:T(8,128)}, f32[384,64]{0,1:T(8,128)}) fusion(f32[64,384]{1,0:T(8,128)S(1)} %get-tuple-element.5, f32[64,384]{1,0:T(8,128)S(1)} %get-tuple-element.4), kind=kLoop, calls=%fused_computation | loop fusion | flops 49152 | bytes 393216 | tf_op jit(solution)/shard_map/mul | solution.py:457

commit v4 on v3

--- a/solution.py
+++ b/solution.py
@@ -13,6 +13,7 @@
 DOWN, UP = 0, 1
 TOK, WIDTH, HID = 512, 6144, 512
 AHEAD = 4
+FIRST = 5
 
 
 def remainder(a, n):
@@ -63,26 +64,27 @@
     for pair in range(8):
         loads.append([
             pltpu.make_async_copy(wup_hbm.at[pl.ds(pair * 768, 768), :], wup.at[pair], load_sem.at[pair]),
-            pltpu.make_async_copy(tok_hbm.at[:, wide(pair, 0)], tok.at[pair, 0], load_sem.at[8 + pair]),
-            pltpu.make_async_copy(tok_hbm.at[:, wide(pair, 1)], tok.at[pair, 1], load_sem.at[8 + pair]),
+            pltpu.make_async_copy(tok_hbm.at[:, wide(pair, 0)], tok.at[pair, 0], load_sem.at[pair]),
+            pltpu.make_async_copy(tok_hbm.at[:, wide(pair, 1)], tok.at[pair, 1], load_sem.at[pair]),
         ])
-    own_loads, other_loads, wdn_loads = [], [], []
+    own_loads, other_loads = [], []
     for i, pair in enumerate(needed):
-        own_loads.append([pltpu.make_async_copy(grad_hbm.at[:, wide(pair, core)], grad.at[pair, core], load_sem.at[16 + i])])
-        other_loads.append([pltpu.make_async_copy(grad_hbm.at[:, wide(pair, 1 - core)], grad.at[pair, 1 - core], load_sem.at[24 + i])])
-        wdn_loads.append([pltpu.make_async_copy(wdn_hbm.at[:, both(pair)], wdn.at[pair], load_sem.at[32 + i])])
-    loads += own_loads
-    for i in range(8):
-        loads.append(other_loads[i] + wdn_loads[i])
+        own_loads.append([
+            pltpu.make_async_copy(grad_hbm.at[:, wide(pair, core)], grad.at[pair, core], load_sem.at[16 if i < FIRST else 17]),
+        ])
+        other_loads.append([
+            pltpu.make_async_copy(grad_hbm.at[:, wide(pair, 1 - core)], grad.at[pair, 1 - core], load_sem.at[8 + i]),
+            pltpu.make_async_copy(wdn_hbm.at[:, both(pair)], wdn.at[pair], load_sem.at[8 + i]),
+        ])
+    loads += own_loads + other_loads
 
     def begin(group):
         for copy in loads[group]:
             copy.start()
 
-    def finish(ref, sem):
-        pltpu.make_async_copy(ref, ref, load_sem.at[sem]).wait()
-
-    sent = []
+    def finish(count, sem):
+        ref = tok_mate.at[pl.ds(0, count)]
+        pltpu.make_async_copy(ref, ref, sem).wait()
 
     def send(source, target, phase, sem, to):
         pltpu.make_async_remote_copy(
@@ -91,65 +93,74 @@
         ).start()
 
     def sem_at(bucket, color, which):
-        return (bucket * 3 + color) * 5 + which
+        return (bucket * 3 + color) * 4 + which
 
     def arrived(ref, bucket, color, which):
         pltpu.make_async_copy(ref, ref, in_sem.at[sem_at(bucket, color, which)]).wait()
 
-    def to_mate(source, target, sem):
-        copy = pltpu.make_async_remote_copy(
-            src_ref=source, dst_ref=target, send_sem=mate_send.at[sem], recv_sem=mate_recv.at[sem],
+    def to_mate(source, target, out, landed):
+        pltpu.make_async_remote_copy(
+            src_ref=source, dst_ref=target, send_sem=mate_send.at[out], recv_sem=mate_recv.at[landed],
             device_id=mate, device_id_type=MESH,
-        )
-        copy.start()
-        sent.append(copy)
-        return copy
-
-    mate_grad = []
+        ).start()
+
 
     def offer(i):
-        mate_grad.append(to_mate(grad_hbm.at[:, wide(needed[i], 1 - core)], grad_mate.at[needed[i]], i))
+        to_mate(grad_hbm.at[:, wide(needed[i], 1 - core)], grad_mate.at[needed[i]], 0, 0 if i < FIRST else 1)
 
     for group in range(AHEAD):
         begin(group)
     with jax.named_scope("barrier"):
         pl.semaphore_wait(barrier, 10)
+    def turn(target, i, value):
+        target[:, :, pl.ds(i * 128, 128)] = value.astype(BF16).T.reshape(8, 64, 128)
+
+    def turn_act(i):
+        p = pre[pl.ds(i * 128, 128), :]
+        turn(act, i, p * (0.5 * (1.0 + lax.erf(p / ROOT2))))
+
+    def turn_hid(i):
+        rows = pl.ds(i * 128, 128)
+        turn(hid, i, lin[rows, :] * pre[rows, :])
+
+    def in_halves(total, product, turned, source, target, out, landed):
+        upper, lower = pl.ds(0, 256), pl.ds(256, 256)
+        total[upper, :] += product(slice(0, 256))
+        piece = product(slice(256, 512))
+        turned(0)
+        turned(1)
+        total[lower, :] += piece
+        to_mate(source.at[:, :, upper], target.at[:, :, upper], out, landed)
+        turned(2)
+        turned(3)
+        to_mate(source.at[:, :, lower], target.at[:, :, lower], out, landed)
+
     for pair in range(8):
         with jax.named_scope(f"preact{pair}"):
-            finish(wup.at[pair], pair)
-            finish(tok.at[pair], 8 + pair)
+            finish(4, load_sem.at[pair])
             begin(pair + AHEAD)
             if pair < 6:
                 offer(pair)
             block = jnp.concatenate([tok[pair, 0], tok[pair, 1]], axis=1)
-            piece = jnp.dot(block, wup[pair], preferred_element_type=F32)
-            pre[...] = piece if pair == 0 else pre[...] + piece
-    for group in range(8 + AHEAD, 18):
-        begin(group)
-
-    def put_turned(target, i, value):
-        target[:, :, pl.ds(pl.multiple_of(i * 128, 128), 128)] = value.astype(BF16).T.reshape(8, 64, 128)
-
-    def halves(source, target, sem, turn):
-        copies = []
-        for half in range(2):
-            @pl.loop(2 * half, 2 * half + 2)
-            def _(i):
-                turn(i)
-
-            lanes = pl.ds(half * 256, 256)
-            copies.append(to_mate(source.at[:, :, lanes], target.at[:, :, lanes], sem + half))
-        return copies
-
-    def turn_act(i):
-        p = pre[pl.ds(pl.multiple_of(i * 128, 128), 128), :]
-        put_turned(act, i, p * (0.5 * (1.0 + lax.erf(p / ROOT2))))
-
-    with jax.named_scope("turn_act"):
-        mate_act = halves(act, act_mate, 9, turn_act)
+            if pair < 7:
+                piece = jnp.dot(block, wup[pair], preferred_element_type=F32)
+                pre[...] = piece if pair == 0 else pre[...] + piece
+            else:
+                for group in range(8 + AHEAD, 18):
+                    begin(group)
+                in_halves(
+                    pre, lambda rows: jnp.dot(block[rows], wup[7], preferred_element_type=F32), turn_act, act, act_mate, 1, 2
+                )
     offer(6)
     offer(7)
-    mate_tok = to_mate(tok.at[:, 1 - core], tok_mate, 8)
+    to_mate(tok.at[:, 1 - core], tok_mate, 2, 3)
+
+    with jax.named_scope("slope"):
+        @pl.loop(0, 4)
+        def _(i):
+            rows = pl.ds(pl.multiple_of(i * 128, 128), 128)
+            p = pre[rows, :]
+            pre[rows, :] = 0.5 * (1.0 + lax.erf(p / ROOT2)) + p * (jnp.exp(-0.5 * p * p) / ROOT2PI)
 
     def term(left, left_mate, right, right_mate, color, shifts, sides=("own", "mate")):
         first = orders[color][0]
@@ -215,13 +226,13 @@
         for color in colors:
             axis = orders[color][0]
             send(part.at[bucket, color, 1, low], far1.at[bucket, color, 0], 0, sem_at(bucket, color, 0), peer(axis, 1))
-            send(part.at[bucket, color, 1, high], far1.at[bucket, color, 1], 0, sem_at(bucket, color, 1), peer(axis, 3))
+            send(part.at[bucket, color, 1, high], far1.at[bucket, color, 1], 0, sem_at(bucket, color, 0), peer(axis, 3))
 
     def send_next(bucket, color, half, phase=0):
-        send(part.at[bucket, color, 0, half], got1.at[bucket, color, 0, half], phase, sem_at(bucket, color, 2), peer(orders[color][0], 1))
+        send(part.at[bucket, color, 0, half], got1.at[bucket, color, 0, half], phase, sem_at(bucket, color, 1), peer(orders[color][0], 1))
 
     def send_last(bucket, color, half, phase=0):
-        send(part.at[bucket, color, 2, half], got1.at[bucket, color, 1, half], phase, sem_at(bucket, color, 2), peer(orders[color][0], 3))
+        send(part.at[bucket, color, 2, half], got1.at[bucket, color, 1, half], phase, sem_at(bucket, color, 1), peer(orders[color][0], 3))
 
     def start_near(bucket, color):
         if color == 1:
@@ -239,19 +250,19 @@
             keep(bucket, color, 0, chunk)
 
     def merge1(bucket, color):
+        arrived(far1.at[bucket, color], bucket, color, 0)
         for side, shift, half, forward in ((0, 1, low, send_next), (1, 3, high, send_last)):
-            arrived(far1.at[bucket, color, side], bucket, color, side)
             part[bucket, color, shift - 1, half] = (
                 part[bucket, color, shift - 1, half].astype(F32) + far1[bucket, color, side].astype(F32)
             ).astype(BF16)
-            forward(bucket, color, half, 3 + bucket * 3 + color)
+            forward(bucket, color, half, 1 if bucket == DOWN else 2 + color)
 
     def merged(bucket, color):
-        pltpu.make_async_copy(part.at[bucket, color, 0], part.at[bucket, color, 0], out_sem.at[3 + bucket * 3 + color]).wait()
+        pltpu.make_async_copy(part.at[bucket, color, 0], part.at[bucket, color, 0], out_sem.at[2 + color]).wait()
 
     def finish1(bucket, color):
         axis = orders[color][1]
-        arrived(got1.at[bucket, color], bucket, color, 2)
+        arrived(got1.at[bucket, color], bucket, color, 1)
 
         def total(shift):
             place = pl.ds(remainder(at[axis] + shift, 4) * 4, 4)
@@ -263,12 +274,12 @@
 
         for shift in (2, 1, 3):
             send2[bucket, color, shift - 1] = total(shift).astype(BF16)
-            send(send2.at[bucket, color, shift - 1], got2.at[bucket, color, shift - 1], 1, sem_at(bucket, color, 3), peer(axis, shift))
+            send(send2.at[bucket, color, shift - 1], got2.at[bucket, color, shift - 1], 5, sem_at(bucket, color, 2), peer(axis, shift))
         own2[bucket, color] = total(0)
 
     def finish2(bucket, color):
         axis = orders[color][2]
-        arrived(got2.at[bucket, color], bucket, color, 3)
+        arrived(got2.at[bucket, color], bucket, color, 2)
 
         def total(place):
             value = own2[bucket, color, place]
@@ -278,11 +289,11 @@
 
         for shift in (2, 1, 3):
             send3[bucket, color, shift - 1] = total(remainder(at[axis] + shift, 4)).astype(BF16)
-            send(send3.at[bucket, color, shift - 1], got3.at[bucket, color, shift - 1], 2, sem_at(bucket, color, 4), peer(axis, shift))
+            send(send3.at[bucket, color, shift - 1], got3.at[bucket, color, shift - 1], 6, sem_at(bucket, color, 3), peer(axis, shift))
         own3[bucket, color] = total(at[axis])
 
     def finish3(bucket, color):
-        arrived(got3.at[bucket, color], bucket, color, 4)
+        arrived(got3.at[bucket, color], bucket, color, 3)
         value = own3[bucket, color]
         for i in range(3):
             value = value + got3[bucket, color, i].astype(F32)
@@ -291,52 +302,40 @@
 
     colors = (2, 0, 1)
 
-    def linear(*order):
-        for i in order:
-            pair = needed[i]
-            finish(grad.at[pair, 1 - core], 24 + i)
-            finish(wdn.at[pair], 32 + i)
-            block = jnp.concatenate([grad[pair, 0], grad[pair, 1]], axis=1)
-            piece = lax.dot_general(block, wdn[pair], (((1,), (1,)), ((), ())), preferred_element_type=F32)
+    def linear(i):
+        pair = needed[i]
+        finish(3, load_sem.at[8 + i])
+        block = jnp.concatenate([grad[pair, 0], grad[pair, 1]], axis=1)
+
+        def product(rows):
+            return lax.dot_general(block[rows], wdn[pair], (((1,), (1,)), ((), ())), preferred_element_type=F32)
+
+        if i == 7:
+            in_halves(lin, product, turn_hid, hid, hid_mate, 3, 4)
+        else:
+            piece = product(slice(0, 512))
             lin[...] = piece if i == 0 else lin[...] + piece
 
-    def ready_grad(*order):
-        for i in order:
-            finish(grad.at[needed[i], core], 16 + i)
-
-    def ready_mate(*order):
-        for i in order:
-            mate_grad[i].wait_recv()
+    def ready_grad(which):
+        finish((FIRST, 8 - FIRST)[which], load_sem.at[16 + which])
+
+    def ready_mate(which):
+        finish((FIRST, 8 - FIRST)[which], mate_recv.at[which])
 
     def ready_act():
-        for copy in mate_act:
-            copy.wait_recv()
+        pltpu.make_async_copy(act_mate, act_mate, mate_recv.at[2]).wait()
         for group in range(18, 24):
             begin(group)
 
-    def turn_hid(i):
-        rows = pl.ds(pl.multiple_of(i * 128, 128), 128)
-        p = pre[rows, :]
-        slope = 0.5 * (1.0 + lax.erf(p / ROOT2)) + p * (jnp.exp(-0.5 * p * p) / ROOT2PI)
-        put_turned(hid, i, lin[rows, :] * slope)
-
-    mate_hid = []
-
-    def turn_all_hid():
-        mate_hid.extend(halves(hid, hid_mate, 11, turn_hid))
-
     def ready_up():
-        mate_tok.wait_recv()
-        for copy in mate_hid:
-            copy.wait_recv()
+        pltpu.make_async_copy(tok_mate, tok_mate, mate_recv.at[3]).wait()
+        pltpu.make_async_copy(hid_mate, hid_mate, mate_recv.at[4]).wait()
 
     def drain():
-        for copy in sent:
-            copy.wait_send()
-        for color in colors:
-            merged(DOWN, color)
-        for phase, ref in enumerate((part.at[:, :, pl.ds(0, 2)], send2, send3)):
-            pltpu.make_async_copy(ref, ref, out_sem.at[phase]).wait()
+        for i, ref in enumerate((grad_mate, act, tok_mate, hid)):
+            pltpu.make_async_copy(ref, ref, mate_send.at[i]).wait()
+        for i, ref in ((0, part.at[:, :, pl.ds(0, 2)]), (1, part.at[DOWN, :, 0]), (5, send2), (6, send3)):
+            pltpu.make_async_copy(ref, ref, out_sem.at[i]).wait()
 
     def one(step, bucket, *colors):
         with jax.named_scope(f"{step.__name__}_{'DU'[bucket]}" + "".join(map(str, colors))):
@@ -350,15 +349,15 @@
         with jax.named_scope(step.__name__ + "_".join(str(a) for a in args)):
             step(*args)
 
-    alone(ready_grad, 0, 1, 2, 3, 4)
+    alone(ready_grad, 0)
     one(early_far, DOWN, 2, 0)
-    alone(ready_grad, 5, 6, 7)
+    alone(ready_grad, 1)
     one(early_far, DOWN, 1)
     alone(linear, 0)
     alone(ready_act)
-    alone(ready_mate, 0, 1, 2, 3, 4)
+    alone(ready_mate, 0)
     one(start_far, DOWN, 2, 0)
-    alone(ready_mate, 5, 6, 7)
+    alone(ready_mate, 1)
     one(start_far, DOWN, 1)
 
     @pl.when(core == 1)
@@ -378,7 +377,6 @@
     alone(linear, 6)
     alone(linear, 7)
     each(merge1, DOWN)
-    alone(turn_all_hid)
     one(early_far, UP, 2, 0)
     one(early_far, UP, 1)
     one(start_own, DOWN, 2, 0)
@@ -444,11 +442,11 @@
             pltpu.VMEM((2, 3, 3, 64, 128), BF16),
             pltpu.VMEM((2, 3, 64, 128), F32),
             pltpu.VMEM((2, 3, 3, 64, 128), BF16),
-            pltpu.SemaphoreType.DMA((40,)),
-            pltpu.SemaphoreType.DMA((13,)),
-            pltpu.SemaphoreType.DMA((13,)),
-            pltpu.SemaphoreType.DMA((9,)),
-            pltpu.SemaphoreType.DMA((30,)),
+            pltpu.SemaphoreType.DMA((18,)),
+            pltpu.SemaphoreType.DMA((4,)),
+            pltpu.SemaphoreType.DMA((5,)),
+            pltpu.SemaphoreType.DMA((7,)),
+            pltpu.SemaphoreType.DMA((24,)),
         ],
         compiler_params=pltpu.CompilerParams(
             collective_id=0, has_side_effects=True, vmem_limit_bytes=66_000_000

time: 46.1 us -> 45.4 us (0.985)
  Pallas kernels: 44.7 us -> 44 us
    pallas_call x1, Pallas kernels: 44.7 us -> 44 us  [local(): pl.pallas_call(kernel, out_shape=(shape, shape), in_specs=[anywhere] * 4,...]
where the time goes in v4:
time: 45.4 us; the launch traced here: 45.3 us
  Pallas kernels  44 us (97%)
  other arithmetic  0.69 us (2%)
  between operations  0.64 us (1%)
    pallas_call x1, Pallas kernels, local(): pl.pallas_call(kernel, out_shape=(shape, shape), in_specs=[anywhere] * 4,...  44 us

profile of v4, /device:TPU:0, one launch (start us, length us, event | category | flops | bytes accessed | tf_op | source)
XLA Modules:
  0.0 45.3 jit_solution(9727379600369361170)
XLA Ops:
  0.6 44.0 %shard_map.59 = (f32[64,384]{1,0:T(8,128)S(1)}, f32[64,384]{1,0:T(8,128)S(1)}) custom-call(bf16[512,6144]{1,0:T(8,128)(2,1)} %tok_hbm.1, bf16[512,6144]{1,0:T(8,128)(2,1)} %grad_hbm.1, bf16[6144,512]{1,0:T(8,128)(2,1)} %wup_hbm.1, bf16[512,6144]{1,0:T(8,128)(2,1)} %wdn_hbm.1), custom_call_target="tpu_custom_call" | custom-call | tf_op jit(solution)/shard_map/pallas_call | solution.py:417
  44.6 0.7 %multiply_bitcast_fusion = (f32[384,64]{0,1:T(8,128)}, f32[384,64]{0,1:T(8,128)}) fusion(f32[64,384]{1,0:T(8,128)S(1)} %get-tuple-element.5, f32[64,384]{1,0:T(8,128)S(1)} %get-tuple-element.4), kind=kLoop, calls=%fused_computation | loop fusion | flops 49152 | bytes 393216 | tf_op jit(solution)/shard_map/mul | solution.py:455

commit v5 on v4

--- a/solution.py
+++ b/solution.py
@@ -25,7 +25,7 @@
     up_ref, dn_ref,
     tok, grad, wup, wdn, tok_mate, grad_mate,
     pre, lin, act, act_mate, hid, hid_mate,
-    part, own1, far1, got1, send2, own2, got2, send3, own3, got3,
+    part, own1, far1, got1, send2, own2, far2, got2, send3, own3, got3,
     load_sem, mate_send, mate_recv, out_sem, in_sem,
 ):
     row, col = lax.axis_index("row"), lax.axis_index("col")
@@ -206,6 +206,7 @@
 
     operands = {DOWN: (act, act_mate, grad, grad_mate), UP: (hid, hid_mate, tok, tok_mate)}
     low, high = pl.ds(0, 8), pl.ds(8, 8)
+    lower, upper = pl.ds(0, 2), pl.ds(2, 2)
 
     def keep(bucket, color, shift, chunk):
         for i, value in chunk.items():
@@ -260,30 +261,53 @@
     def merged(bucket, color):
         pltpu.make_async_copy(part.at[bucket, color, 0], part.at[bucket, color, 0], out_sem.at[2 + color]).wait()
 
+    def total1(bucket, color, shift):
+        place = pl.ds(remainder(at[orders[color][1]] + shift, 4) * 4, 4)
+        return (
+            own1[bucket, color, place]
+            + got1[bucket, color, 0, place].astype(F32)
+            + got1[bucket, color, 1, place].astype(F32)
+        )
+
+    def send_second(bucket, color, source, target, sem, shift):
+        send(source, target, 5, sem, peer(orders[color][1], shift))
+
     def finish1(bucket, color):
-        axis = orders[color][1]
         arrived(got1.at[bucket, color], bucket, color, 1)
-
-        def total(shift):
-            place = pl.ds(remainder(at[axis] + shift, 4) * 4, 4)
-            return (
-                own1[bucket, color, place]
-                + got1[bucket, color, 0, place].astype(F32)
-                + got1[bucket, color, 1, place].astype(F32)
+        sem = sem_at(bucket, color, 2)
+        for shift in (2, 1, 3):
+            out = send2.at[bucket, color, shift - 1]
+            send2[bucket, color, shift - 1] = total1(bucket, color, shift).astype(BF16)
+            if bucket == UP:
+                send_second(bucket, color, out, got2.at[bucket, color, shift - 1], sem, shift)
+            elif shift == 2:
+                send_second(bucket, color, out.at[lower], far2.at[color, 0], 24 + color, 1)
+                send_second(bucket, color, out.at[upper], far2.at[color, 1], 24 + color, 3)
+            elif shift == 1:
+                send_second(bucket, color, out.at[upper], got2.at[bucket, color, 0, upper], sem, 1)
+            else:
+                send_second(bucket, color, out.at[lower], got2.at[bucket, color, 1, lower], sem, 3)
+        own2[bucket, color] = total1(bucket, color, 0)
+
+    def merge2(bucket, color):
+        pltpu.make_async_copy(far2.at[color], far2.at[color], in_sem.at[24 + color]).wait()
+        for side, shift, half in ((0, 1, lower), (1, 3, upper)):
+            send2[bucket, color, shift - 1, half] = (
+                send2[bucket, color, shift - 1, half].astype(F32) + far2[color, side].astype(F32)
+            ).astype(BF16)
+            send_second(
+                bucket, color, send2.at[bucket, color, shift - 1, half], got2.at[bucket, color, side, half],
+                sem_at(bucket, color, 2), shift,
             )
-
-        for shift in (2, 1, 3):
-            send2[bucket, color, shift - 1] = total(shift).astype(BF16)
-            send(send2.at[bucket, color, shift - 1], got2.at[bucket, color, shift - 1], 5, sem_at(bucket, color, 2), peer(axis, shift))
-        own2[bucket, color] = total(0)
 
     def finish2(bucket, color):
         axis = orders[color][2]
-        arrived(got2.at[bucket, color], bucket, color, 2)
+        count = 2 if bucket == DOWN else 3
+        arrived(got2.at[bucket, color, pl.ds(0, count)], bucket, color, 2)
 
         def total(place):
             value = own2[bucket, color, place]
-            for i in range(3):
+            for i in range(count):
                 value = value + got2[bucket, color, i, place].astype(F32)
             return value
 
@@ -401,10 +425,11 @@
         one(merged, UP, (color + 1) % 3)
         one(finish1, DOWN, color)
     each(finish1, UP)
+    each(merge2, DOWN)
+    each(finish2, UP)
     each(finish2, DOWN)
-    each(finish2, UP)
+    each(finish3, UP)
     each(finish3, DOWN)
-    each(finish3, UP)
     alone(drain)
 
 
@@ -438,6 +463,7 @@
             pltpu.VMEM((2, 3, 2, 16, 64, 128), BF16),
             pltpu.VMEM((2, 3, 3, 4, 64, 128), BF16),
             pltpu.VMEM((2, 3, 4, 64, 128), F32),
+            pltpu.VMEM((3, 2, 2, 64, 128), BF16),
             pltpu.VMEM((2, 3, 3, 4, 64, 128), BF16),
             pltpu.VMEM((2, 3, 3, 64, 128), BF16),
             pltpu.VMEM((2, 3, 64, 128), F32),
@@ -446,7 +472,7 @@
             pltpu.SemaphoreType.DMA((4,)),
             pltpu.SemaphoreType.DMA((5,)),
             pltpu.SemaphoreType.DMA((7,)),
-            pltpu.SemaphoreType.DMA((24,)),
+            pltpu.SemaphoreType.DMA((27,)),
         ],
         compiler_params=pltpu.CompilerParams(
             collective_id=0, has_side_effects=True, vmem_limit_bytes=66_000_000

time: 45.4 us -> 44.9 us (0.989)
  Pallas kernels: 44 us -> 43.5 us
    pallas_call x1, Pallas kernels: 44 us -> 43.5 us  [local(): pl.pallas_call(kernel, out_shape=(shape, shape), in_specs=[anywhere] * 4,...]
where the time goes in v5:
time: 44.9 us; the launch traced here: 44.8 us
  Pallas kernels  43.5 us (97%)
  other arithmetic  0.69 us (2%)
  between operations  0.64 us (1%)
    pallas_call x1, Pallas kernels, local(): pl.pallas_call(kernel, out_shape=(shape, shape), in_specs=[anywhere] * 4,...  43.5 us

profile of v5, /device:TPU:0, one launch (start us, length us, event | category | flops | bytes accessed | tf_op | source)
XLA Modules:
  0.0 44.8 jit_solution(6361706619188487355)
XLA Ops:
  0.6 43.5 %shard_map.59 = (f32[64,384]{1,0:T(8,128)S(1)}, f32[64,384]{1,0:T(8,128)S(1)}) custom-call(bf16[512,6144]{1,0:T(8,128)(2,1)} %tok_hbm.1, bf16[512,6144]{1,0:T(8,128)(2,1)} %grad_hbm.1, bf16[6144,512]{1,0:T(8,128)(2,1)} %wup_hbm.1, bf16[512,6144]{1,0:T(8,128)(2,1)} %wdn_hbm.1), custom_call_target="tpu_custom_call" | custom-call | tf_op jit(solution)/shard_map/pallas_call | solution.py:442
  44.1 0.7 %multiply_bitcast_fusion = (f32[384,64]{0,1:T(8,128)}, f32[384,64]{0,1:T(8,128)}) fusion(f32[64,384]{1,0:T(8,128)S(1)} %get-tuple-element.5, f32[64,384]{1,0:T(8,128)S(1)} %get-tuple-element.4), kind=kLoop, calls=%fused_computation | loop fusion | flops 49152 | bytes 393216 | tf_op jit(solution)/shard_map/mul | solution.py:481

commit v6 on v5

--- a/solution.py
+++ b/solution.py
@@ -220,10 +220,19 @@
         for color, chunk in zip(colors, chunks):
             keep(bucket, color, 0, chunk)
 
+    def whole_far(bucket, *colors):
+        chunks = [term(*operands[bucket], color, (2,))[0] for color in colors]
+        for color, chunk in zip(colors, chunks):
+            keep(bucket, color, 2, chunk)
+        send_far(bucket, *colors)
+
     def start_far(bucket, *colors):
         chunks = [term(*operands[bucket], color, (2,), ("mate",))[0] for color in colors]
         for color, chunk in zip(colors, chunks):
             keep(bucket, color, 2, {i: value + own1[bucket, color, i] for i, value in chunk.items()})
+        send_far(bucket, *colors)
+
+    def send_far(bucket, *colors):
         for color in colors:
             axis = orders[color][0]
             send(part.at[bucket, color, 1, low], far1.at[bucket, color, 0], 0, sem_at(bucket, color, 0), peer(axis, 1))
@@ -373,28 +382,36 @@
         with jax.named_scope(step.__name__ + "_".join(str(a) for a in args)):
             step(*args)
 
-    alone(ready_grad, 0)
-    one(early_far, DOWN, 2, 0)
-    alone(ready_grad, 1)
-    one(early_far, DOWN, 1)
-    alone(linear, 0)
-    alone(ready_act)
-    alone(ready_mate, 0)
-    one(start_far, DOWN, 2, 0)
-    alone(ready_mate, 1)
-    one(start_far, DOWN, 1)
-
     @pl.when(core == 1)
     def _():
+        alone(ready_grad, 0)
+        one(early_far, DOWN, 2, 0)
+        alone(ready_grad, 1)
+        one(early_far, DOWN, 1)
+        alone(linear, 0)
+        alone(ready_act)
+        alone(ready_mate, 0)
+        one(start_far, DOWN, 2, 0)
+        alone(linear, 1)
+        alone(ready_mate, 1)
+        one(start_far, DOWN, 1)
+        alone(linear, 2)
+        each(start_near, DOWN)
+
+    @pl.when(core == 0)
+    def _():
+        alone(ready_grad, 0)
+        alone(ready_grad, 1)
+        alone(ready_act)
+        alone(ready_mate, 0)
+        one(whole_far, DOWN, 2, 0)
+        alone(ready_mate, 1)
+        one(whole_far, DOWN, 1)
+        each(start_near, DOWN)
+        alone(linear, 0)
         alone(linear, 1)
         alone(linear, 2)
-        each(start_near, DOWN)
-
-    @pl.when(core == 0)
-    def _():
-        each(start_near, DOWN)
-        alone(linear, 1)
-        alone(linear, 2)
+
     alone(linear, 3)
     alone(linear, 4)
     alone(linear, 5)

time: 44.9 us -> 44.9 us (level)
  no operation moved by 1% of the time
where the time goes in v6:
time: 44.9 us; the launch traced here: 44.7 us
  Pallas kernels  43.4 us (97%)
  other arithmetic  0.69 us (2%)
  between operations  0.64 us (1%)
    pallas_call x1, Pallas kernels, local(): pl.pallas_call(kernel, out_shape=(shape, shape), in_specs=[anywhere] * 4,...  43.4 us

profile of v6, /device:TPU:0, one launch (start us, length us, event | category | flops | bytes accessed | tf_op | source)
XLA Modules:
  0.0 44.7 jit_solution(9145835611522388926)
XLA Ops:
  0.6 43.4 %shard_map.59 = (f32[64,384]{1,0:T(8,128)S(1)}, f32[64,384]{1,0:T(8,128)S(1)}) custom-call(bf16[512,6144]{1,0:T(8,128)(2,1)} %tok_hbm.1, bf16[512,6144]{1,0:T(8,128)(2,1)} %grad_hbm.1, bf16[6144,512]{1,0:T(8,128)(2,1)} %wup_hbm.1, bf16[512,6144]{1,0:T(8,128)(2,1)} %wdn_hbm.1), custom_call_target="tpu_custom_call" | custom-call | tf_op jit(solution)/shard_map/pallas_call | solution.py:459
  44.0 0.7 %multiply_bitcast_fusion = (f32[384,64]{0,1:T(8,128)}, f32[384,64]{0,1:T(8,128)}) fusion(f32[64,384]{1,0:T(8,128)S(1)} %get-tuple-element.5, f32[64,384]{1,0:T(8,128)S(1)} %get-tuple-element.4), kind=kLoop, calls=%fused_computation | loop fusion | flops 49152 | bytes 393216 | tf_op jit(solution)/shard_map/mul | solution.py:498

commit v7 on v6

--- a/solution.py
+++ b/solution.py
@@ -401,14 +401,14 @@
     @pl.when(core == 0)
     def _():
         alone(ready_grad, 0)
-        alone(ready_grad, 1)
         alone(ready_act)
         alone(ready_mate, 0)
         one(whole_far, DOWN, 2, 0)
+        alone(linear, 0)
+        alone(ready_grad, 1)
         alone(ready_mate, 1)
         one(whole_far, DOWN, 1)
         each(start_near, DOWN)
-        alone(linear, 0)
         alone(linear, 1)
         alone(linear, 2)
 
@@ -438,9 +438,18 @@
         one(start_own, UP, 2, 0, 1)
 
     each(merge1, UP)
-    for color in colors:
-        one(merged, UP, (color + 1) % 3)
-        one(finish1, DOWN, color)
+    @pl.when(core == 1)
+    def _():
+        for color in colors:
+            one(merged, UP, (color + 1) % 3)
+            one(finish1, DOWN, color)
+
+    @pl.when(core == 0)
+    def _():
+        each(finish1, DOWN)
+        for color in colors:
+            one(merged, UP, color)
+
     each(finish1, UP)
     each(merge2, DOWN)
     each(finish2, UP)

time: 44.9 us -> 44.9 us (level)
  no operation moved by 1% of the time
where the time goes in v7:
time: 44.9 us; the launch traced here: 44.8 us
  Pallas kernels  43.4 us (97%)
  other arithmetic  0.69 us (2%)
  between operations  0.64 us (1%)
    pallas_call x1, Pallas kernels, local(): pl.pallas_call(kernel, out_shape=(shape, shape), in_specs=[anywhere] * 4,...  43.4 us

profile of v7, /device:TPU:0, one launch (start us, length us, event | category | flops | bytes accessed | tf_op | source)
XLA Modules:
  0.0 44.8 jit_solution(15733942701446849708)
XLA Ops:
  0.6 43.4 %shard_map.59 = (f32[64,384]{1,0:T(8,128)S(1)}, f32[64,384]{1,0:T(8,128)S(1)}) custom-call(bf16[512,6144]{1,0:T(8,128)(2,1)} %tok_hbm.1, bf16[512,6144]{1,0:T(8,128)(2,1)} %grad_hbm.1, bf16[6144,512]{1,0:T(8,128)(2,1)} %wup_hbm.1, bf16[512,6144]{1,0:T(8,128)(2,1)} %wdn_hbm.1), custom_call_target="tpu_custom_call" | custom-call | tf_op jit(solution)/shard_map/pallas_call | solution.py:468
  44.1 0.7 %multiply_bitcast_fusion = (f32[384,64]{0,1:T(8,128)}, f32[384,64]{0,1:T(8,128)}) fusion(f32[64,384]{1,0:T(8,128)S(1)} %get-tuple-element.5, f32[64,384]{1,0:T(8,128)S(1)} %get-tuple-element.4), kind=kLoop, calls=%fused_computation | loop fusion | flops 49152 | bytes 393216 | tf_op jit(solution)/shard_map/mul | solution.py:507
